TPU v7x, 32 devices: a whole 2x2x4 slice. The times are simulated.
32 devices in a mesh: clip: 2 (over y), patch: 4 (over z), head: 2 (over x), rep: 2 (over core).
Axes of the slice: x: 2, y: 2, z: 4, core: 2. Of those that a mesh axis runs over, the one named last changes fastest.
Arguments:
- tokens: bfloat16 [1024, 3072], P(('clip', 'patch', 'head', 'rep')), parts along dimension 0, may hold values from -24 to 24
- modulation: float32 [3, 3072], replicated, may hold values from -3 to 3
- in_weight: bfloat16 [3072, 16, 384], P(None, ('head', 'rep')), may hold values from -0.109375 to 0.109375
- query_gain: float32 [128], replicated, may hold values from 1 to 2.5
- key_gain: float32 [128], replicated, may hold values from 0.25 to 1.75
- out_weight: bfloat16 [16, 128, 3072], P(('head', 'rep')), may hold values from -1.5 to 1.5
- stale_cache: bfloat16 [1024, 16, 256], P(('clip', 'patch', 'head', 'rep')), parts along dimension 0, may hold values from -440 to 440, as said below
- lengths: int32 [8], P('clip'), parts along dimension 0, may hold values from 1 to 128, 384 in all
Outputs:
- update: bfloat16 [1024, 3072], P(('clip', 'patch', 'head', 'rep')), parts along dimension 0
- new_cache: bfloat16 [1024, 16, 256], P(('clip', 'patch', 'head', 'rep')), parts along dimension 0
There are 2 independent parts, one for each index of `clip`. A program takes and returns all parts, laid end to end along the dimension named above; an argument that names none is the same for every part. Nothing has to cross between parts.
Inputs may be any that keep to these rules, and one draw needn't show every extreme that they name: stale_cache[s, h] holds the stale key of token s and head h in its first 128 entries and the stale value in its last 128. Only the first lengths[p] tokens of patch p are live keys.
All inputs are finite; a program needn't handle non-finite values.
Results may differ from a plain program's by a relative error of at most 0.02.
The roundings to bfloat16 on the way count: a program that leaves them out, or rounds other values in their place, can miss the bound.
Values may be sent and summed in bfloat16 or wider, within the bound.
A program may use at most 128 MiB of HBM per device.

v0:
```python
import functools
import math

import jax
import jax.numpy as jnp
from jax import lax
from jax.experimental import pallas as pl
from jax.experimental.pallas import tpu as pltpu
from jax.sharding import PartitionSpec as P

EPSILON = 1e-06
NEGATIVE = -1e30
key_block = 512


def normalize_rows(values):
    average = jnp.mean(values, axis=-1, keepdims=True)
    centred = values - average
    variance = jnp.mean(centred * centred, axis=-1, keepdims=True)
    return centred * lax.rsqrt(variance + EPSILON)


def rms_gain(values, gain):
    return values * lax.rsqrt(jnp.mean(values * values, axis=-1, keepdims=True) + EPSILON) * gain


def project(normed, in_weight, query_gain, key_gain):
    row_count = normed.shape[0]
    head_count = in_weight.shape[1]
    triple = in_weight.shape[2]
    head_dim = triple // 3
    flat_weight = in_weight.reshape(in_weight.shape[0], head_count * triple)
    projected = jnp.dot(normed, flat_weight, preferred_element_type=jnp.float32).reshape(
        row_count, head_count, triple
    )
    queries = rms_gain(projected[..., :head_dim], query_gain)
    fresh_keys = rms_gain(projected[..., head_dim : 2 * head_dim], key_gain)
    return jnp.concatenate([queries, fresh_keys, projected[..., 2 * head_dim :]], axis=-1).astype(
        jnp.bfloat16
    )


def lookup(lengths, patch_of):
    patch_ids = jnp.arange(lengths.shape[0], dtype=jnp.int32)
    return jnp.sum(jnp.where(patch_of[:, None] == patch_ids[None, :], lengths[None, :], 0), axis=1)


def attend(running, queries, key_rows, usable):
    head_dim = queries.shape[-1]
    row_max, denominator, weighted = running
    scores = jnp.einsum(
        "qhd,khd->qhk", queries, key_rows[..., :head_dim], preferred_element_type=jnp.float32
    )
    scores = scores * (1.0 / math.sqrt(head_dim))
    key_mask = usable[None, None, :]
    scores = jnp.where(key_mask, scores, NEGATIVE)
    new_max = jnp.maximum(row_max, jnp.max(scores, axis=-1))
    weights = jnp.where(key_mask, jnp.exp(scores - new_max[..., None]), 0.0)
    factor = jnp.exp(row_max - new_max)
    denominator = denominator * factor + jnp.sum(weights, axis=-1)
    weighted = weighted * factor[..., None] + jnp.einsum(
        "qhk,khd->qhd",
        weights.astype(jnp.bfloat16),
        key_rows[..., head_dim:],
        preferred_element_type=jnp.float32,
    )
    return (new_max, denominator, weighted)


def attend_blocks(running, queries, key_rows, usable):
    key_count = key_rows.shape[0]
    if key_count > key_block and key_count % key_block == 0:
        shaped = key_rows.reshape((key_count // key_block, key_block) + key_rows.shape[1:])
        usable_rows = usable.reshape(key_count // key_block, key_block)

        def step_block(current, operands):
            return (attend(current, queries, operands[0], operands[1]), None)

        running, _ = lax.scan(step_block, running, (shaped, usable_rows))
        return running
    return attend(running, queries, key_rows, usable)


def per_device(
    tokens, modulation, in_weight, query_gain, key_gain, out_weight, stale_cache, lengths
):
    heads_dev = in_weight.shape[1]
    head_dim = query_gain.shape[0]
    normed = (
        normalize_rows(tokens.astype(jnp.float32)) * (1.0 + modulation[1]) + modulation[0]
    ).astype(jnp.bfloat16)
    fresh = project(
        lax.all_gather(normed, ("head", "rep"), axis=0, tiled=True), in_weight, query_gain, key_gain
    )
    queries = fresh[..., :head_dim]
    own_rows = fresh[..., head_dim:]
    new_cache = lax.all_to_all(own_rows, ("head", "rep"), split_axis=0, concat_axis=1, tiled=True)
    patch_tok = fresh.shape[0]
    own_patch = lax.axis_index("patch")
    own_length = lookup(lengths, jnp.full((1,), own_patch, jnp.int32))[0]
    running = (
        jnp.full((patch_tok, heads_dev), NEGATIVE, jnp.float32),
        jnp.zeros((patch_tok, heads_dev), jnp.float32),
        jnp.zeros((patch_tok, heads_dev, head_dim), jnp.float32),
    )
    running = attend_blocks(
        running, queries, own_rows, jnp.arange(patch_tok, dtype=jnp.int32) < own_length
    )
    stale_heads = lax.all_to_all(
        stale_cache, ("head", "rep"), split_axis=1, concat_axis=0, tiled=True
    )
    shard_part = lax.all_gather(stale_heads, "patch", axis=0, tiled=True)
    key_index = jnp.arange(shard_part.shape[0], dtype=jnp.int32)
    patch_of = key_index // patch_tok
    position = key_index % patch_tok
    usable = (position < lookup(lengths, patch_of)) & (patch_of != own_patch)
    running = attend_blocks(running, queries, shard_part, usable)
    attended = (running[2] / running[1][..., None]).astype(jnp.bfloat16)
    flat_rows = attended.reshape(patch_tok, heads_dev * head_dim)
    flat_weight = out_weight.reshape(heads_dev * head_dim, out_weight.shape[2])
    attention = lax.psum_scatter(
        jnp.dot(flat_rows, flat_weight, preferred_element_type=jnp.float32).astype(jnp.bfloat16),
        ("head", "rep"),
        scatter_dimension=0,
        tiled=True,
    ).astype(jnp.float32)
    update = (modulation[2] * attention).astype(jnp.bfloat16)
    return (update, new_cache)


MESH = pl.DeviceIdType.MESH
K_CHUNKS = 4
OUT_CHUNKS = 4


def fused_kernel(
    tok, mod, qg, kg, lens, st, w_hbm, ow_hbm, upd, nc_out,
    w_v, ow_v, normed_all, acc, stale_all, ncbuf, ncrecv, att, pbuf, dbuf, xs, xr,
    w_sem, ow_sem, loc_sem, st_send, st_recv, zs_r, zs_l, z_recv,
    na_s, nb_s, nr_s, n_recv, nc_s, nc_r, d_s, d_r, x_s, x_r,
    *, patches, transposed,
):
    p = lax.axis_index("patch")
    h = lax.axis_index("head")
    r = lax.axis_index("rep")
    heads = ow_hbm.shape[0]
    head_dim = ow_hbm.shape[1]
    rows, width = tok.shape
    triple = 3 * head_dim
    kc = width // K_CHUNKS
    oc = width // OUT_CHUNKS
    group = 4
    patch_tok = group * rows
    coords = [(h, r), (h, 1 - r), (1 - h, r), (1 - h, 1 - r)]
    slot = [a * 2 + b for a, b in coords]
    dev = [{"head": a, "rep": b} for a, b in coords]

    def remote(src, dst, ss, rs, to):
        return pltpu.make_async_remote_copy(
            src_ref=src, dst_ref=dst, send_sem=ss, recv_sem=rs, device_id=to, device_id_type=MESH
        )

    def w_copy(c):
        if transposed:
            return pltpu.make_async_copy(
                w_hbm.at[:, pl.ds(c * kc, kc)], w_v.at[:, pl.ds(c * kc, kc)], w_sem.at[c]
            )
        return pltpu.make_async_copy(
            w_hbm.at[pl.ds(c * kc, kc)], w_v.at[pl.ds(c * kc, kc)], w_sem.at[c]
        )

    for c in range(K_CHUNKS):
        w_copy(c).start()
    ow_copy = pltpu.make_async_copy(ow_hbm, ow_v, ow_sem)
    ow_copy.start()
    own_stale = pltpu.make_async_copy(
        st.at[pl.ds(slot[0] * heads, heads)], stale_all.at[p, slot[0]], loc_sem
    )
    own_stale.start()

    has_right = p + 1 < patches
    has_left = p > 0
    barrier = pltpu.get_barrier_semaphore()
    for k in (1, 2, 3):
        pl.semaphore_signal(barrier, inc=1, device_id=dev[k], device_id_type=MESH)

    @pl.when(has_right)
    def _():
        pl.semaphore_signal(barrier, inc=1, device_id={"patch": p + 1}, device_id_type=MESH)

    @pl.when(has_left)
    def _():
        pl.semaphore_signal(barrier, inc=1, device_id={"patch": p - 1}, device_id_type=MESH)

    values = tok[...].astype(jnp.float32)
    normed = (normalize_rows(values) * (1.0 + mod[1:2, :]) + mod[0:1, :]).astype(jnp.bfloat16)
    normed_all[slot[0]] = normed

    pl.semaphore_wait(barrier, 3 + has_right.astype(jnp.int32) + has_left.astype(jnp.int32))

    def stale_copy(k):
        return remote(
            st.at[pl.ds(slot[k] * heads, heads)], stale_all.at[p, slot[0]],
            st_send.at[k], st_recv.at[k], dev[k],
        )

    def stale_arrival(k):
        place = stale_all.at[p, slot[k]]
        remote(place, place, st_send.at[k], st_recv.at[k], dev[k]).wait_recv()

    def z_copy(q, k, right):
        place = stale_all.at[q, slot[k]]
        if right:
            return remote(place, place, zs_r.at[q, k], z_recv.at[q, k], {"patch": p + 1})
        return remote(place, place, zs_l.at[q, k], z_recv.at[q, k], {"patch": p - 1})

    def z_own(k):
        @pl.when(has_right)
        def _():
            z_copy(p, k, True).start()

        @pl.when(has_left)
        def _():
            z_copy(p, k, False).start()

    def z_relay(d, k):
        @pl.when(p - d >= 0)
        def _():
            z_copy(p - d, k, False).wait_recv()

            @pl.when(has_right)
            def _():
                z_copy(p - d, k, True).start()

        @pl.when(p + d < patches)
        def _():
            z_copy(p + d, k, True).wait_recv()

            @pl.when(has_left)
            def _():
                z_copy(p + d, k, False).start()

    def feature_copy(which, c):
        if which == 1:
            place = normed_all.at[slot[0], :, pl.ds(c * kc, kc)]
            return remote(place, place, na_s.at[c], n_recv.at[1, c], dev[1])
        if which == 2:
            place = normed_all.at[slot[0], :, pl.ds(c * kc, kc)]
            return remote(place, place, nb_s.at[c], n_recv.at[2, c], dev[2])
        place = normed_all.at[slot[2], :, pl.ds(c * kc, kc)]
        return remote(place, place, nr_s.at[c], n_recv.at[3, c], dev[1])

    def feature_arrival(k, c):
        place = normed_all.at[slot[k], :, pl.ds(c * kc, kc)]
        remote(place, place, na_s.at[c], n_recv.at[k, c], dev[1]).wait_recv()

    for k in (1, 2, 3):
        stale_copy(k).start()
    own_stale.wait()
    z_own(0)
    for c in range(K_CHUNKS):
        feature_copy(2, c).start()
        feature_copy(1, c).start()
    stale_arrival(1)
    z_own(1)

    for k in (2, 3):
        stale_arrival(k)
        z_own(k)

    relays = [(d, k) for d in range(1, patches) for k in range(group)]
    early = 2 * K_CHUNKS
    for c in range(K_CHUNKS):
        feature_arrival(2, c)
        feature_copy(3, c).start()
        if c > 0:
            for d, k in relays[2 * (c - 1) : 2 * c]:
                z_relay(d, k)
        w_copy(c).wait()
        feature_arrival(1, c)
        feature_arrival(3, c)
        part = normed_all[:, :, c * kc : (c + 1) * kc].reshape(patch_tok, kc)
        for j in range(heads):
            if transposed:
                w_block = w_v[j, c * kc : (c + 1) * kc, :]
            else:
                w_block = w_v[c * kc : (c + 1) * kc, j, :]
            product = jnp.dot(part, w_block, preferred_element_type=jnp.float32)
            if c == 0:
                acc[j] = product
            else:
                acc[j] += product

    for d, k in relays[early - 2 : early]:
        z_relay(d, k)

    q_gain = qg[...]
    k_gain = kg[...]
    queries = []
    for j in range(heads):
        queries.append(rms_gain(acc[j, :, :head_dim], q_gain).astype(jnp.bfloat16))
        keys = rms_gain(acc[j, :, head_dim : 2 * head_dim], k_gain).astype(jnp.bfloat16)
        ncbuf[:, j, :, :head_dim] = keys.reshape(group, rows, head_dim)
        ncbuf[:, j, :, head_dim:] = (
            acc[j, :, 2 * head_dim :].astype(jnp.bfloat16).reshape(group, rows, head_dim)
        )

    def cache_copy(k):
        return remote(
            ncbuf.at[slot[k]], ncrecv.at[slot[0]], nc_s.at[k], nc_r.at[k], dev[k]
        )

    for k in (2, 3, 1):
        cache_copy(k).start()
    scale = 1.0 / math.sqrt(head_dim)
    own_cols = lax.broadcasted_iota(jnp.int32, (1, patch_tok), 1)
    own_mask = own_cols < lens[p]
    other_mask = jnp.concatenate(
        [(own_cols < jnp.where(p == q, 0, lens[q])).astype(jnp.int32) for q in range(patches)],
        axis=1,
    ) > 0
    contract = (((1,), (1,)), ((), ()))
    own_scores = []
    for j in range(heads):
        own_k = ncbuf[:, j, :, :head_dim].reshape(patch_tok, head_dim)
        own_scores.append(
            lax.dot_general(queries[j], own_k, contract, preferred_element_type=jnp.float32)
        )
    for d, k in relays[early:]:
        z_relay(d, k)
    for j in range(heads):
        own_v = ncbuf[:, j, :, head_dim:].reshape(patch_tok, head_dim)
        far_k = stale_all[:, :, j, :, :head_dim].reshape(patches * patch_tok, head_dim)
        far_v = stale_all[:, :, j, :, head_dim:].reshape(patches * patch_tok, head_dim)
        s_far = lax.dot_general(queries[j], far_k, contract, preferred_element_type=jnp.float32)
        s_own = jnp.where(own_mask, own_scores[j] * scale, NEGATIVE)
        s_far = jnp.where(other_mask, s_far * scale, NEGATIVE)
        top = jnp.maximum(
            jnp.max(s_own, axis=1, keepdims=True), jnp.max(s_far, axis=1, keepdims=True)
        )
        w_own = jnp.where(own_mask, jnp.exp(s_own - top), 0.0)
        w_far = jnp.where(other_mask, jnp.exp(s_far - top), 0.0)
        denominator = jnp.sum(w_own, axis=1, keepdims=True) + jnp.sum(w_far, axis=1, keepdims=True)
        total = jnp.dot(
            w_own.astype(jnp.bfloat16), own_v, preferred_element_type=jnp.float32
        ) + jnp.dot(w_far.astype(jnp.bfloat16), far_v, preferred_element_type=jnp.float32)
        att[:, j * head_dim : (j + 1) * head_dim] = (total / denominator).astype(jnp.bfloat16)

    ow_copy.wait()

    def d_copy(c, i):
        return remote(
            pbuf.at[c, slot[1 + 2 * i]], dbuf.at[c, i], d_s.at[c, i], d_r.at[c, i], dev[1]
        )

    def x_copy(c):
        return remote(xs.at[c], xr.at[c], x_s.at[c], x_r.at[c], dev[2])

    def pair_sum(c):
        d_copy(c, 1).wait_recv()
        xs[c] = (
            pbuf[c, slot[2]].astype(jnp.float32) + dbuf[c, 1].astype(jnp.float32)
        ).astype(jnp.bfloat16)
        x_copy(c).start()

    rows_att = att[...]
    flat = heads * head_dim
    for c in range(OUT_CHUNKS):
        piece = jnp.dot(
            rows_att,
            ow_v[:, :, c * oc : (c + 1) * oc].reshape(flat, oc),
            preferred_element_type=jnp.float32,
        )
        pbuf[c] = piece.astype(jnp.bfloat16).reshape(group, rows, oc)
        d_copy(c, 1).start()
        d_copy(c, 0).start()
        if c > 0:
            pair_sum(c - 1)
    pair_sum(OUT_CHUNKS - 1)

    nc_out[pl.ds(slot[0] * heads, heads)] = ncbuf[slot[0]]
    for k in (1, 2, 3):
        place = ncrecv.at[slot[k]]
        remote(place, place, nc_s.at[k], nc_r.at[k], dev[k]).wait_recv()
        nc_out[pl.ds(slot[k] * heads, heads)] = ncrecv[slot[k]]

    for c in range(OUT_CHUNKS):
        d_copy(c, 0).wait_recv()
        x_copy(c).wait_recv()
        total = (
            pbuf[c, slot[0]].astype(jnp.float32)
            + dbuf[c, 0].astype(jnp.float32)
            + xr[c].astype(jnp.float32)
        )
        upd[:, c * oc : (c + 1) * oc] = (mod[2:3, c * oc : (c + 1) * oc] * total).astype(
            jnp.bfloat16
        )

    for k in (1, 2, 3):
        stale_copy(k).wait_send()
        cache_copy(k).wait_send()
    for c in range(K_CHUNKS):
        for which in (1, 2, 3):
            feature_copy(which, c).wait_send()
    for c in range(OUT_CHUNKS):
        d_copy(c, 0).wait_send()
        d_copy(c, 1).wait_send()
        x_copy(c).wait_send()
    for q in range(patches):
        for k in range(group):

            @pl.when(has_right & (q <= p))
            def _():
                z_copy(q, k, True).wait_send()

            @pl.when(has_left & (q >= p))
            def _():
                z_copy(q, k, False).wait_send()


TRANSPOSED = True


def fused_device(
    patches, tokens, modulation, in_weight, query_gain, key_gain, out_weight, stale_cache, lengths
):
    rows, width = tokens.shape
    heads, head_dim = out_weight.shape[:2]
    group = 4
    all_heads = stale_cache.shape[1]
    patch_tok = rows * group
    bf, f32 = jnp.bfloat16, jnp.float32
    oc = width // OUT_CHUNKS
    vm = pl.BlockSpec(memory_space=pltpu.VMEM)
    anyspace = pl.BlockSpec(memory_space=pl.ANY)
    weight = jnp.transpose(in_weight, (1, 0, 2)) if TRANSPOSED else in_weight
    dma = pltpu.SemaphoreType.DMA
    upd, cache = pl.pallas_call(
        functools.partial(fused_kernel, patches=patches, transposed=TRANSPOSED),
        out_shape=(
            jax.ShapeDtypeStruct((rows, width), bf),
            jax.ShapeDtypeStruct((all_heads, rows, 2 * head_dim), bf),
        ),
        in_specs=[vm, vm, vm, vm, pl.BlockSpec(memory_space=pltpu.SMEM), vm, anyspace, anyspace],
        out_specs=(vm, vm),
        scratch_shapes=[
            pltpu.VMEM(weight.shape, bf),
            pltpu.VMEM(out_weight.shape, bf),
            pltpu.VMEM((group, rows, width), bf),
            pltpu.VMEM((heads, patch_tok, 3 * head_dim), f32),
            pltpu.VMEM((patches, group, heads, rows, 2 * head_dim), bf),
            pltpu.VMEM((group, heads, rows, 2 * head_dim), bf),
            pltpu.VMEM((group, heads, rows, 2 * head_dim), bf),
            pltpu.VMEM((patch_tok, heads * head_dim), bf),
            pltpu.VMEM((OUT_CHUNKS, group, rows, oc), bf),
            pltpu.VMEM((OUT_CHUNKS, 2, rows, oc), bf),
            pltpu.VMEM((OUT_CHUNKS, rows, oc), bf),
            pltpu.VMEM((OUT_CHUNKS, rows, oc), bf),
            dma((K_CHUNKS,)), dma, dma, dma((4,)), dma((4,)),
            dma((patches, 4)), dma((patches, 4)), dma((patches, 4)),
            dma((K_CHUNKS,)), dma((K_CHUNKS,)), dma((K_CHUNKS,)), dma((4, K_CHUNKS)),
            dma((4,)), dma((4,)),
            dma((OUT_CHUNKS, 2)), dma((OUT_CHUNKS, 2)), dma((OUT_CHUNKS,)), dma((OUT_CHUNKS,)),
        ],
        compiler_params=pltpu.CompilerParams(
            collective_id=0, has_side_effects=True, vmem_limit_bytes=56 * 1024 * 1024
        ),
    )(
        tokens, modulation, query_gain.reshape(1, -1), key_gain.reshape(1, -1), lengths,
        jnp.transpose(stale_cache, (1, 0, 2)), weight, out_weight,
    )
    return upd, jnp.transpose(cache, (1, 0, 2))


def choose(
    patches, group_shape, tokens, modulation, in_weight, query_gain, key_gain, out_weight,
    stale_cache, lengths,
):
    rows, width = tokens.shape
    heads, head_dim = out_weight.shape[:2]
    kv_bytes = patches * 4 * heads * rows * 4 * head_dim
    weight_bytes = 2 * (in_weight.size + out_weight.size)
    fits = (
        group_shape == (2, 2)
        and rows % 16 == 0
        and head_dim % 128 == 0
        and width % (128 * K_CHUNKS) == 0
        and width % (128 * OUT_CHUNKS) == 0
        and rows * 4 * patches <= 1024
        and kv_bytes + weight_bytes <= 24 * 1024 * 1024
    )
    args = (
        tokens, modulation, in_weight, query_gain, key_gain, out_weight, stale_cache, lengths
    )
    return fused_device(patches, *args) if fits else per_device(*args)


def solution(mesh):
    return jax.shard_map(
        functools.partial(
            choose, mesh.shape["patch"], (mesh.shape["head"], mesh.shape["rep"])
        ),
        mesh=mesh,
        in_specs=(
            P(("clip", "patch", "head", "rep"), None),
            P(),
            P(None, ("head", "rep"), None),
            P(),
            P(),
            P(("head", "rep"), None, None),
            P(("clip", "patch", "head", "rep"), None, None),
            P("clip"),
        ),
        out_specs=(
            P(("clip", "patch", "head", "rep"), None),
            P(("clip", "patch", "head", "rep"), None, None),
        ),
        check_vma=False,
    )
```

profile of v0, /device:TPU:0, one launch (start us, length us, event | category | flops | bytes accessed | tf_op | source)
XLA Modules:
  0.0 51.3 jit_solution(13404153563373725719)
XLA Ops:
  0.6 1.7 %copy.16 = bf16[32,16,256]{2,0,1:T(8,128)(2,1)} copy(bf16[32,16,256]{2,1,0:T(8,128)(2,1)} %param.14) | data formatting | bytes 524288 | tf_op args[6]
  2.4 8.5 %copy.15 = bf16[3072,4,384]{2,0,1:T(8,128)(2,1)} copy(bf16[3072,4,384]{2,1,0:T(4,128)(2,1)} %param.10) | data formatting | bytes 18874368 | tf_op args[2]
  10.9 37.0 %shard_map.95 = (bf16[32,3072]{1,0:T(8,128)(2,1)}, bf16[16,32,256]{2,1,0:T(8,128)(2,1)}) custom-call(bf16[32,3072]{1,0:T(8,128)(2,1)} %tok.1, f32[3,3072]{1,0:T(4,128)} %mod.1, f32[1,128]{1,0:T(1,128)} %bitcast.12, f32[1,128]{1,0:T(1,128)} %bitcast.13, s32[4]{0:T(128)} %lens.1, bf16[16,32,256]{2,1,0:T(8,128)(2,1)} %bitcast.10, ...), custom_call_target="tpu_custom_call" | custom-call | tf_op jit(solution)/shard_map/pallas_call | solution.py:438
  47.9 1.8 %copy.12 = bf16[32,16,256]{2,1,0:T(8,128)(2,1)} copy(bf16[32,16,256]{2,0,1:T(8,128)(2,1)} %bitcast.11) | data formatting | bytes 524288
  49.7 1.6 %copy.18 = bf16[32,3072]{1,0:T(8,128)(2,1)} copy(bf16[32,3072]{1,0:T(8,128)(2,1)} %get-tuple-element.10) | data formatting | bytes 393216
where the time goes:
time: 51.6 us; the launch traced here: 51.3 us
  Pallas kernels  37 us (72%)
  local copies, waits for them, and re-layouts  13.7 us (27%)
  between operations  0.64 us (1%)
    pallas_call x1, Pallas kernels, fused_device(): pl.pallas_call(functools.partial(fused_kernel, patches=patches, transpose...  37 us
    unnamed x4, local copies, waits for them, and re-layouts  13.7 us

commit v1 on v0

--- a/solution.py
+++ b/solution.py
@@ -135,10 +135,10 @@
 
 def fused_kernel(
     tok, mod, qg, kg, lens, st, w_hbm, ow_hbm, upd, nc_out,
-    w_v, ow_v, normed_all, acc, stale_all, ncbuf, ncrecv, att, pbuf, dbuf, xs, xr,
-    w_sem, ow_sem, loc_sem, st_send, st_recv, zs_r, zs_l, z_recv,
+    w_raw, w_v, ow_v, st_t, normed_all, acc, stale_all, ncbuf, ncrecv, att, pbuf, dbuf, xs, xr,
+    w_sem, ow_sem, st_send, st_recv, zs_r, zs_l, z_recv,
     na_s, nb_s, nr_s, n_recv, nc_s, nc_r, d_s, d_r, x_s, x_r,
-    *, patches, transposed,
+    *, patches,
 ):
     p = lax.axis_index("patch")
     h = lax.axis_index("head")
@@ -161,22 +161,22 @@
         )
 
     def w_copy(c):
-        if transposed:
-            return pltpu.make_async_copy(
-                w_hbm.at[:, pl.ds(c * kc, kc)], w_v.at[:, pl.ds(c * kc, kc)], w_sem.at[c]
-            )
         return pltpu.make_async_copy(
-            w_hbm.at[pl.ds(c * kc, kc)], w_v.at[pl.ds(c * kc, kc)], w_sem.at[c]
-        )
+            w_hbm.at[pl.ds(c * kc, kc)], w_raw.at[pl.ds(c * kc, kc)], w_sem.at[c]
+        )
+
+    def w_turn(c):
+        w_copy(c).wait()
+
+        @pl.loop(0, kc // TURN)
+        def _(i):
+            at = pl.multiple_of(c * kc + i * TURN, TURN)
+            w_v[:, pl.ds(at, TURN)] = jnp.transpose(w_raw[pl.ds(at, TURN)], (1, 0, 2))
 
     for c in range(K_CHUNKS):
         w_copy(c).start()
     ow_copy = pltpu.make_async_copy(ow_hbm, ow_v, ow_sem)
     ow_copy.start()
-    own_stale = pltpu.make_async_copy(
-        st.at[pl.ds(slot[0] * heads, heads)], stale_all.at[p, slot[0]], loc_sem
-    )
-    own_stale.start()
 
     has_right = p + 1 < patches
     has_left = p > 0
@@ -192,6 +192,8 @@
     def _():
         pl.semaphore_signal(barrier, inc=1, device_id={"patch": p - 1}, device_id_type=MESH)
 
+    st_t[...] = jnp.transpose(st[...], (1, 0, 2))
+    stale_all[p, slot[0]] = st_t[pl.ds(slot[0] * heads, heads)]
     values = tok[...].astype(jnp.float32)
     normed = (normalize_rows(values) * (1.0 + mod[1:2, :]) + mod[0:1, :]).astype(jnp.bfloat16)
     normed_all[slot[0]] = normed
@@ -200,7 +202,7 @@
 
     def stale_copy(k):
         return remote(
-            st.at[pl.ds(slot[k] * heads, heads)], stale_all.at[p, slot[0]],
+            st_t.at[pl.ds(slot[k] * heads, heads)], stale_all.at[p, slot[0]],
             st_send.at[k], st_recv.at[k], dev[k],
         )
 
@@ -256,14 +258,13 @@
 
     for k in (1, 2, 3):
         stale_copy(k).start()
-    own_stale.wait()
     z_own(0)
     for c in range(K_CHUNKS):
         feature_copy(2, c).start()
         feature_copy(1, c).start()
     stale_arrival(1)
     z_own(1)
-
+    w_turn(0)
     for k in (2, 3):
         stale_arrival(k)
         z_own(k)
@@ -276,15 +277,13 @@
         if c > 0:
             for d, k in relays[2 * (c - 1) : 2 * c]:
                 z_relay(d, k)
-        w_copy(c).wait()
+        if c > 0:
+            w_turn(c)
         feature_arrival(1, c)
         feature_arrival(3, c)
         part = normed_all[:, :, c * kc : (c + 1) * kc].reshape(patch_tok, kc)
         for j in range(heads):
-            if transposed:
-                w_block = w_v[j, c * kc : (c + 1) * kc, :]
-            else:
-                w_block = w_v[c * kc : (c + 1) * kc, j, :]
+            w_block = w_v[j, c * kc : (c + 1) * kc, :]
             product = jnp.dot(part, w_block, preferred_element_type=jnp.float32)
             if c == 0:
                 acc[j] = product
@@ -378,11 +377,12 @@
             pair_sum(c - 1)
     pair_sum(OUT_CHUNKS - 1)
 
-    nc_out[pl.ds(slot[0] * heads, heads)] = ncbuf[slot[0]]
+    ncrecv[slot[0]] = ncbuf[slot[0]]
     for k in (1, 2, 3):
         place = ncrecv.at[slot[k]]
         remote(place, place, nc_s.at[k], nc_r.at[k], dev[k]).wait_recv()
-        nc_out[pl.ds(slot[k] * heads, heads)] = ncrecv[slot[k]]
+    landed = ncrecv[...].reshape(group * heads, rows, 2 * head_dim)
+    nc_out[...] = jnp.transpose(landed, (1, 0, 2))
 
     for c in range(OUT_CHUNKS):
         d_copy(c, 0).wait_recv()
@@ -418,7 +418,7 @@
                 z_copy(q, k, False).wait_send()
 
 
-TRANSPOSED = True
+TURN = 32
 
 
 def fused_device(
@@ -433,19 +433,20 @@
     oc = width // OUT_CHUNKS
     vm = pl.BlockSpec(memory_space=pltpu.VMEM)
     anyspace = pl.BlockSpec(memory_space=pl.ANY)
-    weight = jnp.transpose(in_weight, (1, 0, 2)) if TRANSPOSED else in_weight
     dma = pltpu.SemaphoreType.DMA
     upd, cache = pl.pallas_call(
-        functools.partial(fused_kernel, patches=patches, transposed=TRANSPOSED),
+        functools.partial(fused_kernel, patches=patches),
         out_shape=(
             jax.ShapeDtypeStruct((rows, width), bf),
-            jax.ShapeDtypeStruct((all_heads, rows, 2 * head_dim), bf),
+            jax.ShapeDtypeStruct((rows, all_heads, 2 * head_dim), bf),
         ),
         in_specs=[vm, vm, vm, vm, pl.BlockSpec(memory_space=pltpu.SMEM), vm, anyspace, anyspace],
         out_specs=(vm, vm),
         scratch_shapes=[
-            pltpu.VMEM(weight.shape, bf),
+            pltpu.VMEM(in_weight.shape, bf),
+            pltpu.VMEM((heads, width, 3 * head_dim), bf),
             pltpu.VMEM(out_weight.shape, bf),
+            pltpu.VMEM((all_heads, rows, 2 * head_dim), bf),
             pltpu.VMEM((group, rows, width), bf),
             pltpu.VMEM((heads, patch_tok, 3 * head_dim), f32),
             pltpu.VMEM((patches, group, heads, rows, 2 * head_dim), bf),
@@ -456,7 +457,7 @@
             pltpu.VMEM((OUT_CHUNKS, 2, rows, oc), bf),
             pltpu.VMEM((OUT_CHUNKS, rows, oc), bf),
             pltpu.VMEM((OUT_CHUNKS, rows, oc), bf),
-            dma((K_CHUNKS,)), dma, dma, dma((4,)), dma((4,)),
+            dma((K_CHUNKS,)), dma, dma((4,)), dma((4,)),
             dma((patches, 4)), dma((patches, 4)), dma((patches, 4)),
             dma((K_CHUNKS,)), dma((K_CHUNKS,)), dma((K_CHUNKS,)), dma((4, K_CHUNKS)),
             dma((4,)), dma((4,)),
@@ -467,9 +468,9 @@
         ),
     )(
         tokens, modulation, query_gain.reshape(1, -1), key_gain.reshape(1, -1), lengths,
-        jnp.transpose(stale_cache, (1, 0, 2)), weight, out_weight,
-    )
-    return upd, jnp.transpose(cache, (1, 0, 2))
+        stale_cache, in_weight, out_weight,
+    )
+    return upd, cache
 
 
 def choose(

time: 51.6 us -> 41 us (0.79)
  local copies, waits for them, and re-layouts: 13.7 us -> 3.29 us
    unnamed x4 -> x2, local copies, waits for them, and re-layouts: 13.7 us -> 3.29 us
where the time goes in v1:
time: 41 us; the launch traced here: 40.9 us
  Pallas kernels  36.9 us (90%)
  local copies, waits for them, and re-layouts  3.29 us (8%)
  between operations  0.64 us (2%)
    pallas_call x1, Pallas kernels, fused_device(): pl.pallas_call(functools.partial(fused_kernel, patches=patches), out_shap...  36.9 us
    unnamed x2, local copies, waits for them, and re-layouts  3.29 us

profile of v1, /device:TPU:0, one launch (start us, length us, event | category | flops | bytes accessed | tf_op | source)
XLA Modules:
  0.0 40.9 jit_solution(8240228591824056382)
XLA Ops:
  0.6 36.9 %shard_map.95 = (bf16[32,3072]{1,0:T(8,128)(2,1)}, bf16[32,16,256]{2,1,0:T(8,128)(2,1)}) custom-call(bf16[32,3072]{1,0:T(8,128)(2,1)} %tok.1, f32[3,3072]{1,0:T(4,128)} %mod.1, f32[1,128]{1,0:T(1,128)} %bitcast.2, f32[1,128]{1,0:T(1,128)} %bitcast.3, s32[4]{0:T(128)} %lens.1, bf16[32,16,256]{2,1,0:T(8,128)(2,1)} %st.1, bf16[3072,4,384]{2,1,0:T(4,128)(2,1)} %w_hbm.1, ...), custom_call_target="tpu_custom_call" | custom-call | tf_op jit(solution)/shard_map/pallas_call | solution.py:437
  37.6 1.6 %copy.12 = bf16[32,3072]{1,0:T(8,128)(2,1)} copy(bf16[32,3072]{1,0:T(8,128)(2,1)} %get-tuple-element.4) | data formatting | bytes 393216
  39.2 1.7 %copy.13 = bf16[32,16,256]{2,1,0:T(8,128)(2,1)} copy(bf16[32,16,256]{2,1,0:T(8,128)(2,1)} %get-tuple-element.5) | data formatting | bytes 524288

commit v2 on v1

--- a/solution.py
+++ b/solution.py
@@ -131,12 +131,23 @@
 MESH = pl.DeviceIdType.MESH
 K_CHUNKS = 4
 OUT_CHUNKS = 4
+TURN = 64
+
+
+def nearest(p, patches, i):
+    place = 0
+    for own in range(patches):
+        others = sorted((q for q in range(patches) if q != own), key=lambda q: (abs(q - own), q))
+        place = place + (p == own).astype(jnp.int32) * others[i]
+    return place
 
 
 def fused_kernel(
-    tok, mod, qg, kg, lens, st, w_hbm, ow_hbm, upd, nc_out,
-    w_raw, w_v, ow_v, st_t, normed_all, acc, stale_all, ncbuf, ncrecv, att, pbuf, dbuf, xs, xr,
-    w_sem, ow_sem, st_send, st_recv, zs_r, zs_l, z_recv,
+    tok_hbm, mod_hbm, qg_hbm, kg_hbm, lens_hbm, st_hbm, w_hbm, ow_hbm, upd, nc_out,
+    tok, mod, qg, kg, lens, st,
+    w_raw, w_v, ow_v, st_t, normed_all, acc, stale_all, ncbuf, ncrecv,
+    qbuf, top_v, den_v, out_v, att, pbuf, dbuf, xs, xr,
+    in_sem, w_sem, ow_sem, st_send, st_recv, zs_r, zs_l, z_recv,
     na_s, nb_s, nr_s, n_recv, nc_s, nc_r, d_s, d_r, x_s, x_r,
     *, patches,
 ):
@@ -160,23 +171,14 @@
             src_ref=src, dst_ref=dst, send_sem=ss, recv_sem=rs, device_id=to, device_id_type=MESH
         )
 
-    def w_copy(c):
-        return pltpu.make_async_copy(
-            w_hbm.at[pl.ds(c * kc, kc)], w_raw.at[pl.ds(c * kc, kc)], w_sem.at[c]
-        )
-
-    def w_turn(c):
-        w_copy(c).wait()
-
-        @pl.loop(0, kc // TURN)
-        def _(i):
-            at = pl.multiple_of(c * kc + i * TURN, TURN)
-            w_v[:, pl.ds(at, TURN)] = jnp.transpose(w_raw[pl.ds(at, TURN)], (1, 0, 2))
-
-    for c in range(K_CHUNKS):
-        w_copy(c).start()
-    ow_copy = pltpu.make_async_copy(ow_hbm, ow_v, ow_sem)
-    ow_copy.start()
+    loads = [
+        pltpu.make_async_copy(src, dst, in_sem.at[i])
+        for i, (src, dst) in enumerate(
+            [(st_hbm, st), (tok_hbm, tok), (mod_hbm, mod), (qg_hbm, qg), (kg_hbm, kg), (lens_hbm, lens)]
+        )
+    ]
+    for load in loads:
+        load.start()
 
     has_right = p + 1 < patches
     has_left = p > 0
@@ -192,38 +194,63 @@
     def _():
         pl.semaphore_signal(barrier, inc=1, device_id={"patch": p - 1}, device_id_type=MESH)
 
+    def w_copy(c):
+        return pltpu.make_async_copy(
+            w_hbm.at[pl.ds(c * kc, kc)], w_raw.at[pl.ds(c * kc, kc)], w_sem.at[c]
+        )
+
+    def w_turn(c):
+        w_copy(c).wait()
+
+        @pl.loop(0, kc // TURN)
+        def _(i):
+            at = pl.multiple_of(c * kc + i * TURN, TURN)
+            turned = jnp.transpose(w_raw[pl.ds(at, TURN)], (1, 0, 2))
+            for j in range(heads):
+                w_v[pl.ds(at, TURN), j * triple : (j + 1) * triple] = turned[j]
+
+    for c in range(K_CHUNKS):
+        w_copy(c).start()
+    ow_copy = pltpu.make_async_copy(ow_hbm, ow_v, ow_sem)
+    ow_copy.start()
+
+    loads[0].wait()
     st_t[...] = jnp.transpose(st[...], (1, 0, 2))
-    stale_all[p, slot[0]] = st_t[pl.ds(slot[0] * heads, heads)]
+    loads[1].wait()
+    loads[2].wait()
     values = tok[...].astype(jnp.float32)
     normed = (normalize_rows(values) * (1.0 + mod[1:2, :]) + mod[0:1, :]).astype(jnp.bfloat16)
     normed_all[slot[0]] = normed
 
     pl.semaphore_wait(barrier, 3 + has_right.astype(jnp.int32) + has_left.astype(jnp.int32))
 
+    def stale_part(k):
+        return st_t.at[pl.ds(slot[k] * heads, heads)]
+
     def stale_copy(k):
         return remote(
-            st_t.at[pl.ds(slot[k] * heads, heads)], stale_all.at[p, slot[0]],
-            st_send.at[k], st_recv.at[k], dev[k],
+            stale_part(k), stale_all.at[p, slot[0]], st_send.at[k], st_recv.at[k], dev[k]
         )
 
     def stale_arrival(k):
         place = stale_all.at[p, slot[k]]
         remote(place, place, st_send.at[k], st_recv.at[k], dev[k]).wait_recv()
 
-    def z_copy(q, k, right):
+    def z_copy(q, k, right, own=False):
         place = stale_all.at[q, slot[k]]
+        src = stale_part(0) if own else place
         if right:
-            return remote(place, place, zs_r.at[q, k], z_recv.at[q, k], {"patch": p + 1})
-        return remote(place, place, zs_l.at[q, k], z_recv.at[q, k], {"patch": p - 1})
+            return remote(src, place, zs_r.at[q, k], z_recv.at[q, k], {"patch": p + 1})
+        return remote(src, place, zs_l.at[q, k], z_recv.at[q, k], {"patch": p - 1})
 
     def z_own(k):
         @pl.when(has_right)
         def _():
-            z_copy(p, k, True).start()
+            z_copy(p, k, True, k == 0).start()
 
         @pl.when(has_left)
         def _():
-            z_copy(p, k, False).start()
+            z_copy(p, k, False, k == 0).start()
 
     def z_relay(d, k):
         @pl.when(p - d >= 0)
@@ -256,53 +283,65 @@
         place = normed_all.at[slot[k], :, pl.ds(c * kc, kc)]
         remote(place, place, na_s.at[c], n_recv.at[k, c], dev[1]).wait_recv()
 
+    relays = [(d, k) for d in range(1, patches) for k in range(group)]
+    done = [0]
+
+    def relay_to(count):
+        for d, k in relays[done[0] : count]:
+            z_relay(d, k)
+        done[0] = max(done[0], count)
+
+    z_own(0)
     for k in (1, 2, 3):
         stale_copy(k).start()
-    z_own(0)
     for c in range(K_CHUNKS):
         feature_copy(2, c).start()
         feature_copy(1, c).start()
     stale_arrival(1)
     z_own(1)
     w_turn(0)
-    for k in (2, 3):
-        stale_arrival(k)
-        z_own(k)
-
-    relays = [(d, k) for d in range(1, patches) for k in range(group)]
-    early = 2 * K_CHUNKS
+    stale_arrival(2)
+    z_own(2)
+    w_turn(1)
+    stale_arrival(3)
+    z_own(3)
+    relay_to(1)
+    for c in range(2, K_CHUNKS):
+        w_turn(c)
+
+    relay_to(2)
+    feature_arrival(2, 0)
+    feature_copy(3, 0).start()
     for c in range(K_CHUNKS):
-        feature_arrival(2, c)
-        feature_copy(3, c).start()
-        if c > 0:
-            for d, k in relays[2 * (c - 1) : 2 * c]:
-                z_relay(d, k)
-        if c > 0:
-            w_turn(c)
+        if c + 1 < K_CHUNKS:
+            feature_arrival(2, c + 1)
+            feature_copy(3, c + 1).start()
         feature_arrival(1, c)
         feature_arrival(3, c)
         part = normed_all[:, :, c * kc : (c + 1) * kc].reshape(patch_tok, kc)
-        for j in range(heads):
-            w_block = w_v[j, c * kc : (c + 1) * kc, :]
-            product = jnp.dot(part, w_block, preferred_element_type=jnp.float32)
-            if c == 0:
-                acc[j] = product
-            else:
-                acc[j] += product
-
-    for d, k in relays[early - 2 : early]:
-        z_relay(d, k)
-
+        product = jnp.dot(
+            part, w_v[c * kc : (c + 1) * kc, :], preferred_element_type=jnp.float32
+        )
+        if c == 0:
+            acc[...] = product
+        else:
+            acc[...] += product
+        relay_to(min(group, 3 + c))
+
+    for load in loads[3:]:
+        load.wait()
     q_gain = qg[...]
     k_gain = kg[...]
-    queries = []
     for j in range(heads):
-        queries.append(rms_gain(acc[j, :, :head_dim], q_gain).astype(jnp.bfloat16))
-        keys = rms_gain(acc[j, :, head_dim : 2 * head_dim], k_gain).astype(jnp.bfloat16)
+        base = j * triple
+        keys = rms_gain(acc[:, base + head_dim : base + 2 * head_dim], k_gain).astype(jnp.bfloat16)
         ncbuf[:, j, :, :head_dim] = keys.reshape(group, rows, head_dim)
         ncbuf[:, j, :, head_dim:] = (
-            acc[j, :, 2 * head_dim :].astype(jnp.bfloat16).reshape(group, rows, head_dim)
-        )
+            acc[:, base + 2 * head_dim : base + triple]
+            .astype(jnp.bfloat16)
+            .reshape(group, rows, head_dim)
+        )
+        qbuf[j] = rms_gain(acc[:, base : base + head_dim], q_gain).astype(jnp.bfloat16)
 
     def cache_copy(k):
         return remote(
@@ -311,39 +350,83 @@
 
     for k in (2, 3, 1):
         cache_copy(k).start()
+    relay_to(group + 1)
     scale = 1.0 / math.sqrt(head_dim)
-    own_cols = lax.broadcasted_iota(jnp.int32, (1, patch_tok), 1)
-    own_mask = own_cols < lens[p]
-    other_mask = jnp.concatenate(
-        [(own_cols < jnp.where(p == q, 0, lens[q])).astype(jnp.int32) for q in range(patches)],
-        axis=1,
-    ) > 0
+    columns = lax.broadcasted_iota(jnp.int32, (1, patch_tok), 1)
     contract = (((1,), (1,)), ((), ()))
-    own_scores = []
-    for j in range(heads):
-        own_k = ncbuf[:, j, :, :head_dim].reshape(patch_tok, head_dim)
-        own_scores.append(
-            lax.dot_general(queries[j], own_k, contract, preferred_element_type=jnp.float32)
-        )
-    for d, k in relays[early:]:
-        z_relay(d, k)
-    for j in range(heads):
-        own_v = ncbuf[:, j, :, head_dim:].reshape(patch_tok, head_dim)
-        far_k = stale_all[:, :, j, :, :head_dim].reshape(patches * patch_tok, head_dim)
-        far_v = stale_all[:, :, j, :, head_dim:].reshape(patches * patch_tok, head_dim)
-        s_far = lax.dot_general(queries[j], far_k, contract, preferred_element_type=jnp.float32)
-        s_own = jnp.where(own_mask, own_scores[j] * scale, NEGATIVE)
-        s_far = jnp.where(other_mask, s_far * scale, NEGATIVE)
-        top = jnp.maximum(
-            jnp.max(s_own, axis=1, keepdims=True), jnp.max(s_far, axis=1, keepdims=True)
-        )
-        w_own = jnp.where(own_mask, jnp.exp(s_own - top), 0.0)
-        w_far = jnp.where(other_mask, jnp.exp(s_far - top), 0.0)
-        denominator = jnp.sum(w_own, axis=1, keepdims=True) + jnp.sum(w_far, axis=1, keepdims=True)
-        total = jnp.dot(
-            w_own.astype(jnp.bfloat16), own_v, preferred_element_type=jnp.float32
-        ) + jnp.dot(w_far.astype(jnp.bfloat16), far_v, preferred_element_type=jnp.float32)
-        att[:, j * head_dim : (j + 1) * head_dim] = (total / denominator).astype(jnp.bfloat16)
+
+    def attend_part(sources, first, last):
+        masks = [columns < live for _, live in sources]
+        scores = [
+            [
+                lax.dot_general(
+                    qbuf[j],
+                    source[:, j, :, :head_dim].reshape(patch_tok, head_dim),
+                    contract,
+                    preferred_element_type=jnp.float32,
+                )
+                for source, _ in sources
+            ]
+            for j in range(heads)
+        ]
+        scores = [
+            [jnp.where(mask, part * scale, NEGATIVE) for part, mask in zip(scores[j], masks)]
+            for j in range(heads)
+        ]
+        tops = [
+            functools.reduce(
+                jnp.maximum, [jnp.max(part, axis=1, keepdims=True) for part in scores[j]]
+            )
+            for j in range(heads)
+        ]
+        if not first:
+            before = [top_v[j] for j in range(heads)]
+            tops = [jnp.maximum(before[j], tops[j]) for j in range(heads)]
+            factor = [jnp.exp(before[j] - tops[j]) for j in range(heads)]
+        weights = [
+            [
+                jnp.where(mask, jnp.exp(part - tops[j]), 0.0)
+                for part, mask in zip(scores[j], masks)
+            ]
+            for j in range(heads)
+        ]
+        mixed = [
+            sum(
+                jnp.dot(
+                    part.astype(jnp.bfloat16),
+                    source[:, j, :, head_dim:].reshape(patch_tok, head_dim),
+                    preferred_element_type=jnp.float32,
+                )
+                for part, (source, _) in zip(weights[j], sources)
+            )
+            for j in range(heads)
+        ]
+        total = [
+            sum(jnp.sum(part, axis=1, keepdims=True) for part in weights[j]) for j in range(heads)
+        ]
+        if not first:
+            total = [total[j] + den_v[j] * factor[j] for j in range(heads)]
+            mixed = [mixed[j] + out_v[j] * factor[j] for j in range(heads)]
+        for j in range(heads):
+            if last:
+                att[:, j * head_dim : (j + 1) * head_dim] = (mixed[j] / total[j]).astype(
+                    jnp.bfloat16
+                )
+            else:
+                top_v[j] = tops[j]
+                den_v[j] = total[j]
+                out_v[j] = mixed[j]
+
+    def other(i):
+        q = nearest(p, patches, i)
+        return stale_all.at[q], lens[q]
+
+    attend_part([(ncbuf, lens[p])], True, False)
+    relay_to(group * (patches - 2))
+    if patches > 2:
+        attend_part([other(i) for i in range(patches - 2)], False, False)
+    relay_to(group * (patches - 1))
+    attend_part([other(patches - 2)], False, True)
 
     ow_copy.wait()
 
@@ -384,6 +467,23 @@
     landed = ncrecv[...].reshape(group * heads, rows, 2 * head_dim)
     nc_out[...] = jnp.transpose(landed, (1, 0, 2))
 
+    for k in (1, 2, 3):
+        stale_copy(k).wait_send()
+        cache_copy(k).wait_send()
+    for c in range(K_CHUNKS):
+        for which in (1, 2, 3):
+            feature_copy(which, c).wait_send()
+    for q in range(patches):
+        for k in range(group):
+
+            @pl.when(has_right & (q <= p))
+            def _():
+                z_copy(q, k, True).wait_send()
+
+            @pl.when(has_left & (q >= p))
+            def _():
+                z_copy(q, k, False).wait_send()
+
     for c in range(OUT_CHUNKS):
         d_copy(c, 0).wait_recv()
         x_copy(c).wait_recv()
@@ -395,30 +495,10 @@
         upd[:, c * oc : (c + 1) * oc] = (mod[2:3, c * oc : (c + 1) * oc] * total).astype(
             jnp.bfloat16
         )
-
-    for k in (1, 2, 3):
-        stale_copy(k).wait_send()
-        cache_copy(k).wait_send()
-    for c in range(K_CHUNKS):
-        for which in (1, 2, 3):
-            feature_copy(which, c).wait_send()
     for c in range(OUT_CHUNKS):
         d_copy(c, 0).wait_send()
         d_copy(c, 1).wait_send()
         x_copy(c).wait_send()
-    for q in range(patches):
-        for k in range(group):
-
-            @pl.when(has_right & (q <= p))
-            def _():
-                z_copy(q, k, True).wait_send()
-
-            @pl.when(has_left & (q >= p))
-            def _():
-                z_copy(q, k, False).wait_send()
-
-
-TURN = 32
 
 
 def fused_device(
@@ -432,45 +512,58 @@
     bf, f32 = jnp.bfloat16, jnp.float32
     oc = width // OUT_CHUNKS
     vm = pl.BlockSpec(memory_space=pltpu.VMEM)
-    anyspace = pl.BlockSpec(memory_space=pl.ANY)
     dma = pltpu.SemaphoreType.DMA
-    upd, cache = pl.pallas_call(
+    return pl.pallas_call(
         functools.partial(fused_kernel, patches=patches),
         out_shape=(
             jax.ShapeDtypeStruct((rows, width), bf),
             jax.ShapeDtypeStruct((rows, all_heads, 2 * head_dim), bf),
         ),
-        in_specs=[vm, vm, vm, vm, pl.BlockSpec(memory_space=pltpu.SMEM), vm, anyspace, anyspace],
+        in_specs=[pl.BlockSpec(memory_space=pltpu.HBM)] * 8,
         out_specs=(vm, vm),
         scratch_shapes=[
+            pltpu.VMEM(tokens.shape, bf),
+            pltpu.VMEM(modulation.shape, f32),
+            pltpu.VMEM((1, head_dim), f32),
+            pltpu.VMEM((1, head_dim), f32),
+            pltpu.SMEM(lengths.shape, jnp.int32),
+            pltpu.VMEM(stale_cache.shape, bf),
             pltpu.VMEM(in_weight.shape, bf),
-            pltpu.VMEM((heads, width, 3 * head_dim), bf),
+            pltpu.VMEM((width, heads * 3 * head_dim), bf),
             pltpu.VMEM(out_weight.shape, bf),
             pltpu.VMEM((all_heads, rows, 2 * head_dim), bf),
             pltpu.VMEM((group, rows, width), bf),
-            pltpu.VMEM((heads, patch_tok, 3 * head_dim), f32),
+            pltpu.VMEM((patch_tok, heads * 3 * head_dim), f32),
             pltpu.VMEM((patches, group, heads, rows, 2 * head_dim), bf),
             pltpu.VMEM((group, heads, rows, 2 * head_dim), bf),
             pltpu.VMEM((group, heads, rows, 2 * head_dim), bf),
+            pltpu.VMEM((heads, patch_tok, head_dim), bf),
+            pltpu.VMEM((heads, patch_tok, 1), f32),
+            pltpu.VMEM((heads, patch_tok, 1), f32),
+            pltpu.VMEM((heads, patch_tok, head_dim), f32),
             pltpu.VMEM((patch_tok, heads * head_dim), bf),
             pltpu.VMEM((OUT_CHUNKS, group, rows, oc), bf),
             pltpu.VMEM((OUT_CHUNKS, 2, rows, oc), bf),
             pltpu.VMEM((OUT_CHUNKS, rows, oc), bf),
             pltpu.VMEM((OUT_CHUNKS, rows, oc), bf),
-            dma((K_CHUNKS,)), dma, dma((4,)), dma((4,)),
+            dma((6,)), dma((K_CHUNKS,)), dma, dma((4,)), dma((4,)),
             dma((patches, 4)), dma((patches, 4)), dma((patches, 4)),
             dma((K_CHUNKS,)), dma((K_CHUNKS,)), dma((K_CHUNKS,)), dma((4, K_CHUNKS)),
             dma((4,)), dma((4,)),
             dma((OUT_CHUNKS, 2)), dma((OUT_CHUNKS, 2)), dma((OUT_CHUNKS,)), dma((OUT_CHUNKS,)),
         ],
         compiler_params=pltpu.CompilerParams(
-            collective_id=0, has_side_effects=True, vmem_limit_bytes=56 * 1024 * 1024
+            collective_id=0, has_side_effects=True, vmem_limit_bytes=48 * 1024 * 1024
         ),
     )(
-        tokens, modulation, query_gain.reshape(1, -1), key_gain.reshape(1, -1), lengths,
-        stale_cache, in_weight, out_weight,
-    )
-    return upd, cache
+        *[
+            pltpu.with_memory_space_constraint(operand, pltpu.HBM)
+            for operand in (
+                tokens, modulation, query_gain.reshape(1, -1), key_gain.reshape(1, -1), lengths,
+                stale_cache, in_weight, out_weight,
+            )
+        ]
+    )
 
 
 def choose(
@@ -487,6 +580,8 @@
         and head_dim % 128 == 0
         and width % (128 * K_CHUNKS) == 0
         and width % (128 * OUT_CHUNKS) == 0
+        and width % (TURN * K_CHUNKS) == 0
+        and patches > 1
         and rows * 4 * patches <= 1024
         and kv_bytes + weight_bytes <= 24 * 1024 * 1024
     )

time: 41 us -> 35 us (0.85)
  Pallas kernels: 36.9 us -> 32.9 us
  local copies, waits for them, and re-layouts: 3.29 us -> 1.38 us
    pallas_call x1, Pallas kernels: 36.9 us -> 32.9 us  [fused_device(): pl.pallas_call(functools.partial(fused_kernel, patches=patches), out_shap...]
    unnamed x2, local copies, waits for them, and re-layouts: 3.29 us -> 1.38 us
where the time goes in v2:
time: 35 us; the launch traced here: 34.9 us
  Pallas kernels  32.9 us (94%)
  local copies, waits for them, and re-layouts  1.38 us (4%)
  between operations  0.64 us (2%)
    pallas_call x1, Pallas kernels, fused_device(): pl.pallas_call(functools.partial(fused_kernel, patches=patches), out_shap...  32.9 us
    unnamed x2, local copies, waits for them, and re-layouts  1.38 us

profile of v2, /device:TPU:0, one launch (start us, length us, event | category | flops | bytes accessed | tf_op | source)
XLA Modules:
  0.0 34.9 jit_solution(14343663244117379155)
XLA Ops:
  0.6 32.9 %shard_map.95 = (bf16[32,3072]{1,0:T(8,128)(2,1)S(1)}, bf16[32,16,256]{2,1,0:T(8,128)(2,1)S(1)}) custom-call(bf16[32,3072]{1,0:T(8,128)(2,1)} %tok_hbm.1, f32[3,3072]{1,0:T(4,128)} %mod_hbm.1, f32[1,128]{1,0:T(1,128)} %bitcast.2, f32[1,128]{1,0:T(1,128)} %bitcast.3, s32[4]{0:T(128)} %lens_hbm.1, bf16[32,16,256]{2,1,0:T(8,128)(2,1)} %st_hbm.1, ...), custom_call_target="tpu_custom_call" | custom-call | tf_op jit(solution)/shard_map/pallas_call | solution.py:516
  33.5 0.7 %copy.12 = bf16[32,3072]{1,0:T(8,128)(2,1)} copy(bf16[32,3072]{1,0:T(8,128)(2,1)S(1)} %get-tuple-element.4) | data formatting | bytes 393216
  34.2 0.7 %copy.13 = bf16[32,16,256]{2,1,0:T(8,128)(2,1)} copy(bf16[32,16,256]{2,1,0:T(8,128)(2,1)S(1)} %get-tuple-element.5) | data formatting | bytes 524288

commit v3 on v2

--- a/solution.py
+++ b/solution.py
@@ -130,7 +130,7 @@
 
 MESH = pl.DeviceIdType.MESH
 K_CHUNKS = 4
-OUT_CHUNKS = 4
+OUT_SPLIT = (3, 4, 5, 6, 6)
 TURN = 64
 
 
@@ -146,9 +146,10 @@
     tok_hbm, mod_hbm, qg_hbm, kg_hbm, lens_hbm, st_hbm, w_hbm, ow_hbm, upd, nc_out,
     tok, mod, qg, kg, lens, st,
     w_raw, w_v, ow_v, st_t, normed_all, acc, stale_all, ncbuf, ncrecv,
-    qbuf, top_v, den_v, out_v, att, pbuf, dbuf, xs, xr,
+    qbuf, top_v, den_v, out_v, att, pbuf, dbuf, raw, xs, xr,
     in_sem, w_sem, ow_sem, st_send, st_recv, zs_r, zs_l, z_recv,
-    na_s, nb_s, nr_s, n_recv, nc_s, nc_r, d_s, d_r, x_s, x_r,
+    na_s, nb_s, nr_s, na_r, nb_r, nr_r, nc_s, nc_r,
+    d_s, d_r, e_s, e_r, raw_s, raw_r, x_s, x_r,
     *, patches,
 ):
     p = lax.axis_index("patch")
@@ -159,7 +160,6 @@
     rows, width = tok.shape
     triple = 3 * head_dim
     kc = width // K_CHUNKS
-    oc = width // OUT_CHUNKS
     group = 4
     patch_tok = group * rows
     coords = [(h, r), (h, 1 - r), (1 - h, r), (1 - h, 1 - r)]
@@ -216,108 +216,110 @@
 
     loads[0].wait()
     st_t[...] = jnp.transpose(st[...], (1, 0, 2))
+
+    pl.semaphore_wait(barrier, 3 + has_right.astype(jnp.int32) + has_left.astype(jnp.int32))
+
+    def stale_part(k):
+        return st_t.at[pl.ds(slot[k] * heads, heads)]
+
+    def stale_copy(k):
+        return remote(
+            stale_part(k), stale_all.at[p, slot[0]], st_send, st_recv.at[k - 1], dev[k]
+        )
+
+    def stale_arrival(k):
+        place = stale_all.at[p, slot[k]]
+        remote(place, place, st_send, st_recv.at[k - 1], dev[k]).wait_recv()
+
+    def z_copy(q, k, right, own=False):
+        place = stale_all.at[q, slot[k]]
+        src = stale_part(0) if own else place
+        if right:
+            return remote(src, place, zs_r.at[q], z_recv.at[q, k], {"patch": p + 1})
+        return remote(src, place, zs_l.at[q], z_recv.at[q, k], {"patch": p - 1})
+
+    def z_own(k):
+        @pl.when(has_right)
+        def _():
+            z_copy(p, k, True, k == 0).start()
+
+        @pl.when(has_left)
+        def _():
+            z_copy(p, k, False, k == 0).start()
+
+    def z_relay(d, k):
+        @pl.when(p - d >= 0)
+        def _():
+            z_copy(p - d, k, False).wait_recv()
+
+            @pl.when(has_right)
+            def _():
+                z_copy(p - d, k, True).start()
+
+        @pl.when(p + d < patches)
+        def _():
+            z_copy(p + d, k, True).wait_recv()
+
+            @pl.when(has_left)
+            def _():
+                z_copy(p + d, k, False).start()
+
+    def chunk(k, c):
+        return normed_all.at[slot[k], :, pl.ds(c * kc, kc)]
+
+    def feature_across(c):
+        return remote(chunk(0, c), chunk(0, c), nb_s, nb_r.at[c], dev[2])
+
+    def feature_beside():
+        place = normed_all.at[slot[0]]
+        return remote(place, place, na_s, na_r, dev[1])
+
+    def feature_relay(c):
+        return remote(chunk(2, c), chunk(2, c), nr_s, nr_r.at[c], dev[1])
+
+    def feature_pass(c):
+        remote(chunk(2, c), chunk(2, c), nb_s, nb_r.at[c], dev[2]).wait_recv()
+        feature_relay(c).start()
+
+    relays = [(d, k) for d in range(1, patches) for k in range(group)]
+    done = [0]
+
+    def relay_to(count):
+        for d, k in relays[done[0] : count]:
+            z_relay(d, k)
+        done[0] = max(done[0], count)
+
+    z_own(0)
+    for k in (2, 3, 1):
+        stale_copy(k).start()
     loads[1].wait()
     loads[2].wait()
     values = tok[...].astype(jnp.float32)
     normed = (normalize_rows(values) * (1.0 + mod[1:2, :]) + mod[0:1, :]).astype(jnp.bfloat16)
     normed_all[slot[0]] = normed
-
-    pl.semaphore_wait(barrier, 3 + has_right.astype(jnp.int32) + has_left.astype(jnp.int32))
-
-    def stale_part(k):
-        return st_t.at[pl.ds(slot[k] * heads, heads)]
-
-    def stale_copy(k):
-        return remote(
-            stale_part(k), stale_all.at[p, slot[0]], st_send.at[k], st_recv.at[k], dev[k]
-        )
-
-    def stale_arrival(k):
-        place = stale_all.at[p, slot[k]]
-        remote(place, place, st_send.at[k], st_recv.at[k], dev[k]).wait_recv()
-
-    def z_copy(q, k, right, own=False):
-        place = stale_all.at[q, slot[k]]
-        src = stale_part(0) if own else place
-        if right:
-            return remote(src, place, zs_r.at[q, k], z_recv.at[q, k], {"patch": p + 1})
-        return remote(src, place, zs_l.at[q, k], z_recv.at[q, k], {"patch": p - 1})
-
-    def z_own(k):
-        @pl.when(has_right)
-        def _():
-            z_copy(p, k, True, k == 0).start()
-
-        @pl.when(has_left)
-        def _():
-            z_copy(p, k, False, k == 0).start()
-
-    def z_relay(d, k):
-        @pl.when(p - d >= 0)
-        def _():
-            z_copy(p - d, k, False).wait_recv()
-
-            @pl.when(has_right)
-            def _():
-                z_copy(p - d, k, True).start()
-
-        @pl.when(p + d < patches)
-        def _():
-            z_copy(p + d, k, True).wait_recv()
-
-            @pl.when(has_left)
-            def _():
-                z_copy(p + d, k, False).start()
-
-    def feature_copy(which, c):
-        if which == 1:
-            place = normed_all.at[slot[0], :, pl.ds(c * kc, kc)]
-            return remote(place, place, na_s.at[c], n_recv.at[1, c], dev[1])
-        if which == 2:
-            place = normed_all.at[slot[0], :, pl.ds(c * kc, kc)]
-            return remote(place, place, nb_s.at[c], n_recv.at[2, c], dev[2])
-        place = normed_all.at[slot[2], :, pl.ds(c * kc, kc)]
-        return remote(place, place, nr_s.at[c], n_recv.at[3, c], dev[1])
-
-    def feature_arrival(k, c):
-        place = normed_all.at[slot[k], :, pl.ds(c * kc, kc)]
-        remote(place, place, na_s.at[c], n_recv.at[k, c], dev[1]).wait_recv()
-
-    relays = [(d, k) for d in range(1, patches) for k in range(group)]
-    done = [0]
-
-    def relay_to(count):
-        for d, k in relays[done[0] : count]:
-            z_relay(d, k)
-        done[0] = max(done[0], count)
-
-    z_own(0)
-    for k in (1, 2, 3):
-        stale_copy(k).start()
     for c in range(K_CHUNKS):
-        feature_copy(2, c).start()
-        feature_copy(1, c).start()
+        feature_across(c).start()
+    feature_beside().start()
     stale_arrival(1)
     z_own(1)
     w_turn(0)
+    w_turn(1)
     stale_arrival(2)
     z_own(2)
-    w_turn(1)
+    w_turn(2)
     stale_arrival(3)
     z_own(3)
     relay_to(1)
-    for c in range(2, K_CHUNKS):
+    for c in range(3, K_CHUNKS):
         w_turn(c)
-
     relay_to(2)
-    feature_arrival(2, 0)
-    feature_copy(3, 0).start()
+    feature_pass(0)
+    beside = normed_all.at[slot[1]]
+    remote(beside, beside, na_s, na_r, dev[1]).wait_recv()
     for c in range(K_CHUNKS):
         if c + 1 < K_CHUNKS:
-            feature_arrival(2, c + 1)
-            feature_copy(3, c + 1).start()
-        feature_arrival(1, c)
-        feature_arrival(3, c)
+            feature_pass(c + 1)
+        remote(chunk(3, c), chunk(3, c), nr_s, nr_r.at[c], dev[1]).wait_recv()
         part = normed_all[:, :, c * kc : (c + 1) * kc].reshape(patch_tok, kc)
         product = jnp.dot(
             part, w_v[c * kc : (c + 1) * kc, :], preferred_element_type=jnp.float32
@@ -345,7 +347,7 @@
 
     def cache_copy(k):
         return remote(
-            ncbuf.at[slot[k]], ncrecv.at[slot[0]], nc_s.at[k], nc_r.at[k], dev[k]
+            ncbuf.at[slot[k]], ncrecv.at[slot[0]], nc_s, nc_r, dev[k]
         )
 
     for k in (2, 3, 1):
@@ -430,75 +432,98 @@
 
     ow_copy.wait()
 
-    def d_copy(c, i):
-        return remote(
-            pbuf.at[c, slot[1 + 2 * i]], dbuf.at[c, i], d_s.at[c, i], d_r.at[c, i], dev[1]
-        )
+    cuts = []
+    for units in OUT_SPLIT:
+        begin = cuts[-1].stop if cuts else 0
+        cuts.append(slice(begin, begin + units * (width // sum(OUT_SPLIT))))
+    ranges = [pl.ds(cut.start, cut.stop - cut.start) for cut in cuts]
+
+    def near_copy(c):
+        cols = ranges[c]
+        return remote(pbuf.at[slot[1], :, cols], dbuf.at[0, :, cols], d_s, d_r, dev[1])
+
+    def pair_copy(c):
+        cols = ranges[c]
+        return remote(pbuf.at[slot[3], :, cols], dbuf.at[1, :, cols], e_s, e_r.at[c - 1], dev[1])
+
+    def raw_copy(k):
+        cols = ranges[0]
+        return remote(pbuf.at[slot[k], :, cols], raw.at[k - 2], raw_s, raw_r, dev[k])
 
     def x_copy(c):
-        return remote(xs.at[c], xr.at[c], x_s.at[c], x_r.at[c], dev[2])
-
-    def pair_sum(c):
-        d_copy(c, 1).wait_recv()
-        xs[c] = (
-            pbuf[c, slot[2]].astype(jnp.float32) + dbuf[c, 1].astype(jnp.float32)
+        cols = ranges[c]
+        return remote(xs.at[:, cols], xr.at[:, cols], x_s, x_r.at[c - 1], dev[2])
+
+    rows_att = att[...]
+    flat = heads * head_dim
+    for c, cut in enumerate(cuts):
+        piece = jnp.dot(
+            rows_att,
+            ow_v[:, :, cut].reshape(flat, cut.stop - cut.start),
+            preferred_element_type=jnp.float32,
+        )
+        pbuf[:, :, cut] = piece.astype(jnp.bfloat16).reshape(group, rows, cut.stop - cut.start)
+        if c == 0:
+            raw_copy(2).start()
+            raw_copy(3).start()
+        else:
+            pair_copy(c).start()
+        near_copy(c).start()
+    for c in range(1, len(cuts)):
+        pair_copy(c).wait_recv()
+        cut = cuts[c]
+        xs[:, cut] = (
+            pbuf[slot[2], :, cut].astype(jnp.float32) + dbuf[1, :, cut].astype(jnp.float32)
         ).astype(jnp.bfloat16)
         x_copy(c).start()
 
-    rows_att = att[...]
-    flat = heads * head_dim
-    for c in range(OUT_CHUNKS):
-        piece = jnp.dot(
-            rows_att,
-            ow_v[:, :, c * oc : (c + 1) * oc].reshape(flat, oc),
-            preferred_element_type=jnp.float32,
-        )
-        pbuf[c] = piece.astype(jnp.bfloat16).reshape(group, rows, oc)
-        d_copy(c, 1).start()
-        d_copy(c, 0).start()
-        if c > 0:
-            pair_sum(c - 1)
-    pair_sum(OUT_CHUNKS - 1)
-
     ncrecv[slot[0]] = ncbuf[slot[0]]
-    for k in (1, 2, 3):
-        place = ncrecv.at[slot[k]]
-        remote(place, place, nc_s.at[k], nc_r.at[k], dev[k]).wait_recv()
+    three = ncrecv.at[pl.ds(0, group - 1)]
+    remote(three, three, nc_s, nc_r, dev[1]).wait_recv()
     landed = ncrecv[...].reshape(group * heads, rows, 2 * head_dim)
     nc_out[...] = jnp.transpose(landed, (1, 0, 2))
 
-    for k in (1, 2, 3):
-        stale_copy(k).wait_send()
-        cache_copy(k).wait_send()
-    for c in range(K_CHUNKS):
-        for which in (1, 2, 3):
-            feature_copy(which, c).wait_send()
+    sent = st_t.at[pl.ds(0, (group - 1) * heads)]
+    remote(sent, sent, st_send, st_recv.at[0], dev[1]).wait_send()
+    remote(three, three, nc_s, nc_r, dev[1]).wait_send()
+    for sem in (na_s, nb_s, nr_s):
+        remote(beside, beside, sem, na_r, dev[1]).wait_send()
     for q in range(patches):
-        for k in range(group):
-
-            @pl.when(has_right & (q <= p))
-            def _():
-                z_copy(q, k, True).wait_send()
-
-            @pl.when(has_left & (q >= p))
-            def _():
-                z_copy(q, k, False).wait_send()
-
-    for c in range(OUT_CHUNKS):
-        d_copy(c, 0).wait_recv()
-        x_copy(c).wait_recv()
-        total = (
-            pbuf[c, slot[0]].astype(jnp.float32)
-            + dbuf[c, 0].astype(jnp.float32)
-            + xr[c].astype(jnp.float32)
-        )
-        upd[:, c * oc : (c + 1) * oc] = (mod[2:3, c * oc : (c + 1) * oc] * total).astype(
-            jnp.bfloat16
-        )
-    for c in range(OUT_CHUNKS):
-        d_copy(c, 0).wait_send()
-        d_copy(c, 1).wait_send()
-        x_copy(c).wait_send()
+        whole = stale_all.at[q]
+
+        @pl.when(has_right & (q <= p))
+        def _():
+            remote(whole, whole, zs_r.at[q], z_recv.at[q, 0], {"patch": p + 1}).wait_send()
+
+        @pl.when(has_left & (q >= p))
+        def _():
+            remote(whole, whole, zs_l.at[q], z_recv.at[q, 0], {"patch": p - 1}).wait_send()
+
+    near = dbuf.at[0]
+    remote(near, near, d_s, d_r, dev[1]).wait_recv()
+    remote(raw, raw, raw_s, raw_r, dev[2]).wait_recv()
+    for c, cut in enumerate(cuts):
+        total = pbuf[slot[0], :, cut].astype(jnp.float32) + dbuf[0, :, cut].astype(jnp.float32)
+        if c == 0:
+            total = total + raw[0].astype(jnp.float32) + raw[1].astype(jnp.float32)
+        else:
+            x_copy(c).wait_recv()
+            total = total + xr[:, cut].astype(jnp.float32)
+        upd[:, cut] = (mod[2:3, cut] * total).astype(jnp.bfloat16)
+    remote(near, near, d_s, d_r, dev[1]).wait_send()
+    remote(raw, raw, raw_s, raw_r, dev[2]).wait_send()
+    rest = pl.ds(cuts[1].start, width - cuts[1].start)
+    remote(dbuf.at[1, :, rest], dbuf.at[1, :, rest], e_s, e_r.at[0], dev[1]).wait_send()
+    remote(xs.at[:, rest], xs.at[:, rest], x_s, x_r.at[0], dev[2]).wait_send()
+
+
+def store_kernel(upd, cache, upd_out, cache_out, sems):
+    first = pltpu.make_async_copy(upd, upd_out, sems.at[0])
+    second = pltpu.make_async_copy(cache, cache_out, sems.at[1])
+    first.start()
+    second.start()
+    first.wait()
+    second.wait()
 
 
 def fused_device(
@@ -510,10 +535,11 @@
     all_heads = stale_cache.shape[1]
     patch_tok = rows * group
     bf, f32 = jnp.bfloat16, jnp.float32
-    oc = width // OUT_CHUNKS
+    raw_cols = OUT_SPLIT[0] * (width // sum(OUT_SPLIT))
+    later = len(OUT_SPLIT) - 1
     vm = pl.BlockSpec(memory_space=pltpu.VMEM)
     dma = pltpu.SemaphoreType.DMA
-    return pl.pallas_call(
+    upd, cache = pl.pallas_call(
         functools.partial(fused_kernel, patches=patches),
         out_shape=(
             jax.ShapeDtypeStruct((rows, width), bf),
@@ -542,15 +568,15 @@
             pltpu.VMEM((heads, patch_tok, 1), f32),
             pltpu.VMEM((heads, patch_tok, head_dim), f32),
             pltpu.VMEM((patch_tok, heads * head_dim), bf),
-            pltpu.VMEM((OUT_CHUNKS, group, rows, oc), bf),
-            pltpu.VMEM((OUT_CHUNKS, 2, rows, oc), bf),
-            pltpu.VMEM((OUT_CHUNKS, rows, oc), bf),
-            pltpu.VMEM((OUT_CHUNKS, rows, oc), bf),
-            dma((6,)), dma((K_CHUNKS,)), dma, dma((4,)), dma((4,)),
-            dma((patches, 4)), dma((patches, 4)), dma((patches, 4)),
-            dma((K_CHUNKS,)), dma((K_CHUNKS,)), dma((K_CHUNKS,)), dma((4, K_CHUNKS)),
-            dma((4,)), dma((4,)),
-            dma((OUT_CHUNKS, 2)), dma((OUT_CHUNKS, 2)), dma((OUT_CHUNKS,)), dma((OUT_CHUNKS,)),
+            pltpu.VMEM((group, rows, width), bf),
+            pltpu.VMEM((2, rows, width), bf),
+            pltpu.VMEM((2, rows, raw_cols), bf),
+            pltpu.VMEM((rows, width), bf),
+            pltpu.VMEM((rows, width), bf),
+            dma((6,)), dma((K_CHUNKS,)), dma, dma, dma((3,)),
+            dma((patches,)), dma((patches,)), dma((patches, 4)),
+            dma, dma, dma, dma, dma((K_CHUNKS,)), dma((K_CHUNKS,)), dma, dma,
+            dma, dma, dma, dma((later,)), dma, dma, dma, dma((later,)),
         ],
         compiler_params=pltpu.CompilerParams(
             collective_id=0, has_side_effects=True, vmem_limit_bytes=48 * 1024 * 1024
@@ -564,6 +590,17 @@
             )
         ]
     )
+    return pl.pallas_call(
+        store_kernel,
+        out_shape=(
+            jax.ShapeDtypeStruct(upd.shape, upd.dtype),
+            jax.ShapeDtypeStruct(cache.shape, cache.dtype),
+        ),
+        in_specs=[vm, vm],
+        out_specs=[pl.BlockSpec(memory_space=pltpu.HBM)] * 2,
+        scratch_shapes=[dma((2,))],
+        compiler_params=pltpu.CompilerParams(vmem_limit_bytes=4 * 1024 * 1024),
+    )(upd, cache)
 
 
 def choose(
@@ -579,7 +616,7 @@
         and rows % 16 == 0
         and head_dim % 128 == 0
         and width % (128 * K_CHUNKS) == 0
-        and width % (128 * OUT_CHUNKS) == 0
+        and width % (128 * sum(OUT_SPLIT)) == 0
         and width % (TURN * K_CHUNKS) == 0
         and patches > 1
         and rows * 4 * patches <= 1024

time: 35 us -> 33.5 us (0.957)
  local copies, waits for them, and re-layouts: 1.38 us -> 0 us
    unnamed x2 -> x0, local copies, waits for them, and re-layouts: 1.38 us -> none
    pallas_call x1, Pallas kernels: 32.9 us -> 31.9 us  [fused_device(): pl.pallas_call(functools.partial(fused_kernel, patches=patches), out_shap...]
    pallas_call x0 -> x1, Pallas kernels: none -> 0.79 us  [fused_device(): pl.pallas_call(store_kernel, out_shape=(jax.ShapeDtypeStruct(upd.shape, u...]
where the time goes in v3:
time: 33.5 us; the launch traced here: 33.3 us
  Pallas kernels  32.7 us (98%)
  between operations  0.64 us (2%)
    pallas_call x1, Pallas kernels, fused_device(): pl.pallas_call(functools.partial(fused_kernel, patches=patches), out_shap...  31.9 us
    pallas_call x1, Pallas kernels, fused_device(): pl.pallas_call(store_kernel, out_shape=(jax.ShapeDtypeStruct(upd.shape, u...  0.79 us

profile of v3, /device:TPU:0, one launch (start us, length us, event | category | flops | bytes accessed | tf_op | source)
XLA Modules:
  0.0 33.3 jit_solution(652702224488343540)
XLA Ops:
  0.6 31.9 %shard_map.95 = (bf16[32,3072]{1,0:T(8,128)(2,1)S(1)}, bf16[32,16,256]{2,1,0:T(8,128)(2,1)S(1)}) custom-call(bf16[32,3072]{1,0:T(8,128)(2,1)} %tok_hbm.1, f32[3,3072]{1,0:T(4,128)} %mod_hbm.1, f32[1,128]{1,0:T(1,128)} %bitcast.2, f32[1,128]{1,0:T(1,128)} %bitcast.3, s32[4]{0:T(128)} %lens_hbm.1, bf16[32,16,256]{2,1,0:T(8,128)(2,1)} %st_hbm.1, ...), custom_call_target="tpu_custom_call" | custom-call | tf_op jit(solution)/shard_map/pallas_call | solution.py:542
  32.5 0.8 %shard_map.96 = (bf16[32,3072]{1,0:T(8,128)(2,1)}, bf16[32,16,256]{2,1,0:T(8,128)(2,1)}) custom-call(bf16[32,3072]{1,0:T(8,128)(2,1)S(1)} %get-tuple-element.4.upd, bf16[32,16,256]{2,1,0:T(8,128)(2,1)S(1)} %get-tuple-element.5.cache), custom_call_target="tpu_custom_call" | custom-call | tf_op jit(solution)/shard_map/pallas_call | solution.py:593

commit v4 on v3

--- a/solution.py
+++ b/solution.py
@@ -132,6 +132,8 @@
 K_CHUNKS = 4
 OUT_SPLIT = (3, 4, 5, 6, 6)
 TURN = 64
+SHIP = 1
+RELAYS = (1, 2, 4, 5, 6, 6, 7)
 
 
 def nearest(p, patches, i):
@@ -147,9 +149,10 @@
     tok, mod, qg, kg, lens, st,
     w_raw, w_v, ow_v, st_t, normed_all, acc, stale_all, ncbuf, ncrecv,
     qbuf, top_v, den_v, out_v, att, pbuf, dbuf, raw, xs, xr,
+    guest_q, guest_o, guest_n, home_o, home_n,
     in_sem, w_sem, ow_sem, st_send, st_recv, zs_r, zs_l, z_recv,
     na_s, nb_s, nr_s, na_r, nb_r, nr_r, nc_s, nc_r,
-    d_s, d_r, e_s, e_r, raw_s, raw_r, x_s, x_r,
+    d_s, d_r, e_s, e_r, raw_s, raw_r, x_s, x_r, gq_s, gq_r, go_s, go_r, gn_s, gn_r,
     *, patches,
 ):
     p = lax.axis_index("patch")
@@ -216,6 +219,7 @@
 
     loads[0].wait()
     st_t[...] = jnp.transpose(st[...], (1, 0, 2))
+    stale_all[p, slot[0], 0:SHIP] = st_t[pl.ds(slot[0] * heads, SHIP)]
 
     pl.semaphore_wait(barrier, 3 + has_right.astype(jnp.int32) + has_left.astype(jnp.int32))
 
@@ -231,38 +235,55 @@
         place = stale_all.at[p, slot[k]]
         remote(place, place, st_send, st_recv.at[k - 1], dev[k]).wait_recv()
 
-    def z_copy(q, k, right, own=False):
-        place = stale_all.at[q, slot[k]]
-        src = stale_part(0) if own else place
+    first_end, last_end = p == 0, p == patches - 1
+    to_last, to_first = p == patches - 2, p == 1
+
+    def z_copy(q, k, right, outer, own=False):
+        keep = SHIP if outer else 0
+        place = stale_all.at[q, slot[k], pl.ds(keep, heads - keep)]
+        src = st_t.at[pl.ds(slot[0] * heads + keep, heads - keep)] if own else place
         if right:
             return remote(src, place, zs_r.at[q], z_recv.at[q, k], {"patch": p + 1})
         return remote(src, place, zs_l.at[q], z_recv.at[q, k], {"patch": p - 1})
 
+    def z_send(q, k, right, own=False):
+        edge = to_last if right else to_first
+        inside = (p < patches - 2) if right else (p > 1)
+
+        @pl.when(edge)
+        def _():
+            z_copy(q, k, right, True, own).start()
+
+        @pl.when(inside)
+        def _():
+            z_copy(q, k, right, False, own).start()
+
     def z_own(k):
-        @pl.when(has_right)
+        z_send(p, k, True, k == 0)
+        z_send(p, k, False, k == 0)
+
+    def z_relay(d, k):
+        @pl.when((p - d >= 0) & (p < patches - 1))
         def _():
-            z_copy(p, k, True, k == 0).start()
-
-        @pl.when(has_left)
+            z_copy(p - d, k, False, False).wait_recv()
+            z_send(p - d, k, True)
+
+        @pl.when((p + d < patches) & (p > 0))
         def _():
-            z_copy(p, k, False, k == 0).start()
-
-    def z_relay(d, k):
-        @pl.when(p - d >= 0)
-        def _():
-            z_copy(p - d, k, False).wait_recv()
-
-            @pl.when(has_right)
-            def _():
-                z_copy(p - d, k, True).start()
-
-        @pl.when(p + d < patches)
-        def _():
-            z_copy(p + d, k, True).wait_recv()
-
-            @pl.when(has_left)
-            def _():
-                z_copy(p + d, k, False).start()
+            z_copy(p + d, k, True, False).wait_recv()
+            z_send(p + d, k, False)
+
+    def end_arrivals(distances):
+        for d in distances:
+            for k in range(group):
+
+                @pl.when((p - d >= 0) & last_end)
+                def _():
+                    z_copy(p - d, k, False, True).wait_recv()
+
+                @pl.when((p + d < patches) & first_end)
+                def _():
+                    z_copy(p + d, k, True, True).wait_recv()
 
     def chunk(k, c):
         return normed_all.at[slot[k], :, pl.ds(c * kc, kc)]
@@ -281,7 +302,8 @@
         remote(chunk(2, c), chunk(2, c), nb_s, nb_r.at[c], dev[2]).wait_recv()
         feature_relay(c).start()
 
-    relays = [(d, k) for d in range(1, patches) for k in range(group)]
+    relays = [(1, 0), (1, 1), (1, 2), (2, 0), (2, 1), (1, 3), (2, 2), (2, 3)]
+    relays += [(d, k) for d in range(3, patches - 1) for k in range(group)]
     done = [0]
 
     def relay_to(count):
@@ -304,15 +326,15 @@
     z_own(1)
     w_turn(0)
     w_turn(1)
+    relay_to(RELAYS[0])
     stale_arrival(2)
     z_own(2)
     w_turn(2)
+    relay_to(RELAYS[1])
     stale_arrival(3)
     z_own(3)
-    relay_to(1)
     for c in range(3, K_CHUNKS):
         w_turn(c)
-    relay_to(2)
     feature_pass(0)
     beside = normed_all.at[slot[1]]
     remote(beside, beside, na_s, na_r, dev[1]).wait_recv()
@@ -328,12 +350,31 @@
             acc[...] = product
         else:
             acc[...] += product
-        relay_to(min(group, 3 + c))
+        relay_to(RELAYS[2 + c])
 
     for load in loads[3:]:
         load.wait()
     q_gain = qg[...]
     k_gain = kg[...]
+    def query_of(j):
+        base = j * triple
+        qbuf[j] = rms_gain(acc[:, base : base + head_dim], q_gain).astype(jnp.bfloat16)
+
+    for j in range(SHIP):
+        query_of(j)
+    leaving = qbuf.at[pl.ds(0, SHIP)]
+
+    def guest_copy(step):
+        return remote(leaving, guest_q, gq_s, gq_r, {"patch": p + step})
+
+    @pl.when(first_end)
+    def _():
+        guest_copy(1).start()
+
+    @pl.when(last_end)
+    def _():
+        guest_copy(-1).start()
+
     for j in range(heads):
         base = j * triple
         keys = rms_gain(acc[:, base + head_dim : base + 2 * head_dim], k_gain).astype(jnp.bfloat16)
@@ -343,7 +384,8 @@
             .astype(jnp.bfloat16)
             .reshape(group, rows, head_dim)
         )
-        qbuf[j] = rms_gain(acc[:, base : base + head_dim], q_gain).astype(jnp.bfloat16)
+        if j >= SHIP:
+            query_of(j)
 
     def cache_copy(k):
         return remote(
@@ -352,48 +394,48 @@
 
     for k in (2, 3, 1):
         cache_copy(k).start()
-    relay_to(group + 1)
+    relay_to(RELAYS[2 + K_CHUNKS])
     scale = 1.0 / math.sqrt(head_dim)
     columns = lax.broadcasted_iota(jnp.int32, (1, patch_tok), 1)
     contract = (((1,), (1,)), ((), ()))
 
-    def attend_part(sources, first, last):
+    def attend_part(sources, used, asking, first, finish):
         masks = [columns < live for _, live in sources]
-        scores = [
-            [
+        scores = {
+            j: [
                 lax.dot_general(
-                    qbuf[j],
+                    asking[j],
                     source[:, j, :, :head_dim].reshape(patch_tok, head_dim),
                     contract,
                     preferred_element_type=jnp.float32,
                 )
                 for source, _ in sources
             ]
-            for j in range(heads)
-        ]
-        scores = [
-            [jnp.where(mask, part * scale, NEGATIVE) for part, mask in zip(scores[j], masks)]
-            for j in range(heads)
-        ]
-        tops = [
-            functools.reduce(
+            for j in used
+        }
+        scores = {
+            j: [jnp.where(mask, part * scale, NEGATIVE) for part, mask in zip(scores[j], masks)]
+            for j in used
+        }
+        tops = {
+            j: functools.reduce(
                 jnp.maximum, [jnp.max(part, axis=1, keepdims=True) for part in scores[j]]
             )
-            for j in range(heads)
-        ]
+            for j in used
+        }
         if not first:
-            before = [top_v[j] for j in range(heads)]
-            tops = [jnp.maximum(before[j], tops[j]) for j in range(heads)]
-            factor = [jnp.exp(before[j] - tops[j]) for j in range(heads)]
-        weights = [
-            [
+            before = {j: top_v[j] for j in used}
+            tops = {j: jnp.maximum(before[j], tops[j]) for j in used}
+            factor = {j: jnp.exp(before[j] - tops[j]) for j in used}
+        weights = {
+            j: [
                 jnp.where(mask, jnp.exp(part - tops[j]), 0.0)
                 for part, mask in zip(scores[j], masks)
             ]
-            for j in range(heads)
-        ]
-        mixed = [
-            sum(
+            for j in used
+        }
+        mixed = {
+            j: sum(
                 jnp.dot(
                     part.astype(jnp.bfloat16),
                     source[:, j, :, head_dim:].reshape(patch_tok, head_dim),
@@ -401,34 +443,93 @@
                 )
                 for part, (source, _) in zip(weights[j], sources)
             )
-            for j in range(heads)
-        ]
-        total = [
-            sum(jnp.sum(part, axis=1, keepdims=True) for part in weights[j]) for j in range(heads)
-        ]
+            for j in used
+        }
+        total = {
+            j: sum(jnp.sum(part, axis=1, keepdims=True) for part in weights[j]) for j in used
+        }
         if not first:
-            total = [total[j] + den_v[j] * factor[j] for j in range(heads)]
-            mixed = [mixed[j] + out_v[j] * factor[j] for j in range(heads)]
-        for j in range(heads):
-            if last:
-                att[:, j * head_dim : (j + 1) * head_dim] = (mixed[j] / total[j]).astype(
-                    jnp.bfloat16
-                )
-            else:
-                top_v[j] = tops[j]
-                den_v[j] = total[j]
-                out_v[j] = mixed[j]
-
-    def other(i):
-        q = nearest(p, patches, i)
+            total = {j: total[j] + den_v[j] * factor[j] for j in used}
+            mixed = {j: mixed[j] + out_v[j] * factor[j] for j in used}
+        for j in used:
+            finish(j, tops[j], total[j], mixed[j])
+
+    def keep_part(j, top, total, mixed):
+        top_v[j] = top
+        den_v[j] = total
+        out_v[j] = mixed
+
+    def put_result(j, top, total, mixed):
+        att[:, j * head_dim : (j + 1) * head_dim] = (mixed / total).astype(jnp.bfloat16)
+
+    def other(owner, i):
+        q = nearest(owner, patches, i)
         return stale_all.at[q], lens[q]
 
-    attend_part([(ncbuf, lens[p])], True, False)
-    relay_to(group * (patches - 2))
-    if patches > 2:
-        attend_part([other(i) for i in range(patches - 2)], False, False)
-    relay_to(group * (patches - 1))
-    attend_part([other(patches - 2)], False, True)
+    every = list(range(heads))
+    kept = list(range(SHIP, heads))
+    shipped = list(range(SHIP))
+    is_end = first_end | last_end
+    is_host = to_first | to_last
+    lane = lax.broadcasted_iota(jnp.int32, (patch_tok, head_dim), 1)
+    home = to_last.astype(jnp.int32) * (patches - 1)
+
+    def back_copies(to):
+        return (
+            remote(guest_o, home_o, go_s, go_r, {"patch": to}),
+            remote(guest_n, home_n, gn_s, gn_r, {"patch": to}),
+        )
+
+    def put_guest(j, top, total, mixed):
+        guest_o[j] = (mixed / total).astype(jnp.bfloat16)
+        notes = jnp.where(lane == 0, top, jnp.where(lane == 1, total, 0.0))
+        guest_n[j] = jnp.transpose(notes, (1, 0))[0:8]
+
+    attend_part([(ncbuf, lens[p])], every, qbuf, True, keep_part)
+    relay_to(len(relays))
+
+    @pl.when(is_host)
+    def _():
+        guest_copy(0).wait_recv()
+        sources = [other(home, i) for i in range(patches - 1)]
+        attend_part(sources, shipped, guest_q, True, put_guest)
+        for back in back_copies(home):
+            back.start()
+
+
+    @pl.when(p * (patches - 1 - p) > 0)
+    def _():
+        sources = [other(p, i) for i in range(patches - 1)]
+        attend_part(sources, every, qbuf, False, put_result)
+
+    @pl.when(is_end)
+    def _():
+        end_arrivals(range(1, patches - 1))
+        sources = [other(p, i) for i in range(patches - 2)]
+        attend_part(sources, kept, qbuf, False, keep_part)
+
+    end_arrivals([patches - 1])
+
+    @pl.when(is_end)
+    def _():
+        attend_part([other(p, patches - 2)], kept, qbuf, False, put_result)
+
+
+    @pl.when(is_end)
+    def _():
+        for back in back_copies(home):
+            back.wait_recv()
+        for j in shipped:
+            notes = jnp.concatenate(
+                [home_n[j], jnp.zeros((patch_tok - 8, patch_tok), jnp.float32)], axis=0
+            )
+            notes = jnp.transpose(notes, (1, 0))
+            top, total = notes[:, 0:1], notes[:, 1:2]
+            highest = jnp.maximum(top, top_v[j])
+            away = total * jnp.exp(top - highest)
+            here = jnp.exp(top_v[j] - highest)
+            mixed = home_o[j].astype(jnp.float32) * away + out_v[j] * here
+            put_result(j, highest, away + den_v[j] * here, mixed)
 
     ow_copy.wait()
 
@@ -490,14 +591,32 @@
         remote(beside, beside, sem, na_r, dev[1]).wait_send()
     for q in range(patches):
         whole = stale_all.at[q]
-
-        @pl.when(has_right & (q <= p))
+        outer = stale_all.at[q, :, pl.ds(SHIP, heads - SHIP)]
+
+        @pl.when((p < patches - 2) & (q <= p))
         def _():
             remote(whole, whole, zs_r.at[q], z_recv.at[q, 0], {"patch": p + 1}).wait_send()
 
-        @pl.when(has_left & (q >= p))
+        @pl.when(to_last & (q <= p))
+        def _():
+            remote(outer, outer, zs_r.at[q], z_recv.at[q, 0], {"patch": p + 1}).wait_send()
+
+        @pl.when((p > 1) & (q >= p))
         def _():
             remote(whole, whole, zs_l.at[q], z_recv.at[q, 0], {"patch": p - 1}).wait_send()
+
+        @pl.when(to_first & (q >= p))
+        def _():
+            remote(outer, outer, zs_l.at[q], z_recv.at[q, 0], {"patch": p - 1}).wait_send()
+
+    @pl.when(is_end)
+    def _():
+        guest_copy(0).wait_send()
+
+    @pl.when(is_host)
+    def _():
+        for back in back_copies(home):
+            back.wait_send()
 
     near = dbuf.at[0]
     remote(near, near, d_s, d_r, dev[1]).wait_recv()
@@ -573,10 +692,16 @@
             pltpu.VMEM((2, rows, raw_cols), bf),
             pltpu.VMEM((rows, width), bf),
             pltpu.VMEM((rows, width), bf),
+            pltpu.VMEM((SHIP, patch_tok, head_dim), bf),
+            pltpu.VMEM((SHIP, patch_tok, head_dim), bf),
+            pltpu.VMEM((SHIP, 8, patch_tok), f32),
+            pltpu.VMEM((SHIP, patch_tok, head_dim), bf),
+            pltpu.VMEM((SHIP, 8, patch_tok), f32),
             dma((6,)), dma((K_CHUNKS,)), dma, dma, dma((3,)),
             dma((patches,)), dma((patches,)), dma((patches, 4)),
             dma, dma, dma, dma, dma((K_CHUNKS,)), dma((K_CHUNKS,)), dma, dma,
             dma, dma, dma, dma((later,)), dma, dma, dma, dma((later,)),
+            dma, dma, dma, dma, dma, dma,
         ],
         compiler_params=pltpu.CompilerParams(
             collective_id=0, has_side_effects=True, vmem_limit_bytes=48 * 1024 * 1024
@@ -618,7 +743,9 @@
         and width % (128 * K_CHUNKS) == 0
         and width % (128 * sum(OUT_SPLIT)) == 0
         and width % (TURN * K_CHUNKS) == 0
-        and patches > 1
+        and patches > 3
+        and heads > SHIP
+        and rows * 4 == head_dim
         and rows * 4 * patches <= 1024
         and kv_bytes + weight_bytes <= 24 * 1024 * 1024
     )

time: 33.5 us -> 31.8 us (0.949)
  Pallas kernels: 32.7 us -> 31 us
    pallas_call x1, Pallas kernels: 31.9 us -> 30.3 us  [fused_device(): pl.pallas_call(functools.partial(fused_kernel, patches=patches), out_shap...]
where the time goes in v4:
time: 31.8 us; the launch traced here: 31.7 us
  Pallas kernels  31 us (97%)
  between operations  0.64 us (2%)
    pallas_call x1, Pallas kernels, fused_device(): pl.pallas_call(functools.partial(fused_kernel, patches=patches), out_shap...  30.3 us
    pallas_call x1, Pallas kernels, fused_device(): pl.pallas_call(store_kernel, out_shape=(jax.ShapeDtypeStruct(upd.shape, u...  0.79 us

profile of v4, /device:TPU:0, one launch (start us, length us, event | category | flops | bytes accessed | tf_op | source)
XLA Modules:
  0.0 31.7 jit_solution(15745514845313938098)
XLA Ops:
  0.6 30.3 %shard_map.95 = (bf16[32,3072]{1,0:T(8,128)(2,1)S(1)}, bf16[32,16,256]{2,1,0:T(8,128)(2,1)S(1)}) custom-call(bf16[32,3072]{1,0:T(8,128)(2,1)} %tok_hbm.1, f32[3,3072]{1,0:T(4,128)} %mod_hbm.1, f32[1,128]{1,0:T(1,128)} %bitcast.2, f32[1,128]{1,0:T(1,128)} %bitcast.3, s32[4]{0:T(128)} %lens_hbm.1, bf16[32,16,256]{2,1,0:T(8,128)(2,1)} %st_hbm.1, ...), custom_call_target="tpu_custom_call" | custom-call | tf_op jit(solution)/shard_map/pallas_call | solution.py:661
  30.9 0.8 %shard_map.96 = (bf16[32,3072]{1,0:T(8,128)(2,1)}, bf16[32,16,256]{2,1,0:T(8,128)(2,1)}) custom-call(bf16[32,3072]{1,0:T(8,128)(2,1)S(1)} %get-tuple-element.4.upd, bf16[32,16,256]{2,1,0:T(8,128)(2,1)S(1)} %get-tuple-element.5.cache), custom_call_target="tpu_custom_call" | custom-call | tf_op jit(solution)/shard_map/pallas_call | solution.py:718

commit v5 on v4

--- a/solution.py
+++ b/solution.py
@@ -133,7 +133,8 @@
 OUT_SPLIT = (3, 4, 5, 6, 6)
 TURN = 64
 SHIP = 1
-RELAYS = (1, 2, 4, 5, 6, 6, 7)
+RELAY_ORDER = ((1, 0), (1, 1), (1, 2), (2, 0), (2, 1), (1, 3), (1, 4), (2, 2), (2, 3), (2, 4))
+RELAYS = (1, 2, 4, 5, 7, 7, 8)
 
 
 def nearest(p, patches, i):
@@ -152,7 +153,7 @@
     guest_q, guest_o, guest_n, home_o, home_n,
     in_sem, w_sem, ow_sem, st_send, st_recv, zs_r, zs_l, z_recv,
     na_s, nb_s, nr_s, na_r, nb_r, nr_r, nc_s, nc_r,
-    d_s, d_r, e_s, e_r, raw_s, raw_r, x_s, x_r, gq_s, gq_r, go_s, go_r, gn_s, gn_r,
+    d_s, d_r, e_s, e_r, raw_s, raw_r, x_s, x_r, far_s, gq_s, gq_r, go_s, go_r, gn_s, gn_r,
     *, patches,
 ):
     p = lax.axis_index("patch")
@@ -238,23 +239,34 @@
     first_end, last_end = p == 0, p == patches - 1
     to_last, to_first = p == patches - 2, p == 1
 
+    def landing(q, step, k):
+        return z_recv.at[(q - p - step + patches) % patches - 1, k]
+
     def z_copy(q, k, right, outer, own=False):
-        keep = SHIP if outer else 0
-        place = stale_all.at[q, slot[k], pl.ds(keep, heads - keep)]
-        src = st_t.at[pl.ds(slot[0] * heads + keep, heads - keep)] if own else place
+        begin = SHIP if outer or k == 4 else 0
+        end = SHIP if k == 3 else heads
+        place = stale_all.at[q, slot[min(k, 3)], pl.ds(begin, end - begin)]
+        src = place
+        if own and k == 0:
+            src = st_t.at[pl.ds(slot[0] * heads + begin, end - begin)]
         if right:
-            return remote(src, place, zs_r.at[q], z_recv.at[q, k], {"patch": p + 1})
-        return remote(src, place, zs_l.at[q], z_recv.at[q, k], {"patch": p - 1})
+            return remote(src, place, zs_r.at[q], landing(q, 1, k), {"patch": p + 1})
+        return remote(src, place, zs_l.at[q], landing(q, -1, k), {"patch": p - 1})
+
+    def z_landed(q, k, outer):
+        begin = SHIP if outer or k == 4 else 0
+        end = SHIP if k == 3 else heads
+        place = stale_all.at[q, slot[min(k, 3)], pl.ds(begin, end - begin)]
+        remote(place, place, far_s, landing(q, 0, k), dev[1]).wait_recv()
 
     def z_send(q, k, right, own=False):
-        edge = to_last if right else to_first
-        inside = (p < patches - 2) if right else (p > 1)
-
-        @pl.when(edge)
-        def _():
-            z_copy(q, k, right, True, own).start()
-
-        @pl.when(inside)
+        if k != 3:
+
+            @pl.when(to_last if right else to_first)
+            def _():
+                z_copy(q, k, right, True, own).start()
+
+        @pl.when((p < patches - 2) if right else (p > 1))
         def _():
             z_copy(q, k, right, False, own).start()
 
@@ -262,28 +274,46 @@
         z_send(p, k, True, k == 0)
         z_send(p, k, False, k == 0)
 
+    def z_straight(right):
+        q = 0 if right else patches - 1
+        place = stale_all.at[q, slot[3], pl.ds(SHIP, heads - SHIP)]
+        step = 2 if right else -2
+        return remote(place, place, far_s, landing(q, step, 4), {"patch": p + step})
+
     def z_relay(d, k):
         @pl.when((p - d >= 0) & (p < patches - 1))
         def _():
-            z_copy(p - d, k, False, False).wait_recv()
-            z_send(p - d, k, True)
+            z_landed(p - d, k, False)
+            if (d, k) != (2, 4):
+                z_send(p - d, k, True)
 
         @pl.when((p + d < patches) & (p > 0))
         def _():
-            z_copy(p + d, k, True, False).wait_recv()
-            z_send(p + d, k, False)
+            z_landed(p + d, k, False)
+            if (d, k) != (2, 4):
+                z_send(p + d, k, False)
+
+        if (d, k) == (1, 4):
+
+            @pl.when(to_first)
+            def _():
+                z_straight(True).start()
+
+            @pl.when(to_last)
+            def _():
+                z_straight(False).start()
 
     def end_arrivals(distances):
         for d in distances:
-            for k in range(group):
+            for k in (0, 1, 2, 4):
 
                 @pl.when((p - d >= 0) & last_end)
                 def _():
-                    z_copy(p - d, k, False, True).wait_recv()
+                    z_landed(p - d, k, True)
 
                 @pl.when((p + d < patches) & first_end)
                 def _():
-                    z_copy(p + d, k, True, True).wait_recv()
+                    z_landed(p + d, k, True)
 
     def chunk(k, c):
         return normed_all.at[slot[k], :, pl.ds(c * kc, kc)]
@@ -302,8 +332,7 @@
         remote(chunk(2, c), chunk(2, c), nb_s, nb_r.at[c], dev[2]).wait_recv()
         feature_relay(c).start()
 
-    relays = [(1, 0), (1, 1), (1, 2), (2, 0), (2, 1), (1, 3), (2, 2), (2, 3)]
-    relays += [(d, k) for d in range(3, patches - 1) for k in range(group)]
+    relays = RELAY_ORDER
     done = [0]
 
     def relay_to(count):
@@ -333,6 +362,7 @@
     relay_to(RELAYS[1])
     stale_arrival(3)
     z_own(3)
+    z_own(4)
     for c in range(3, K_CHUNKS):
         w_turn(c)
     feature_pass(0)
@@ -486,7 +516,7 @@
         guest_n[j] = jnp.transpose(notes, (1, 0))[0:8]
 
     attend_part([(ncbuf, lens[p])], every, qbuf, True, keep_part)
-    relay_to(len(relays))
+    relay_to(len(relays) - 1)
 
     @pl.when(is_host)
     def _():
@@ -496,6 +526,7 @@
         for back in back_copies(home):
             back.start()
 
+    relay_to(len(relays))
 
     @pl.when(p * (patches - 1 - p) > 0)
     def _():
@@ -597,7 +628,7 @@
         def _():
             remote(whole, whole, zs_r.at[q], z_recv.at[q, 0], {"patch": p + 1}).wait_send()
 
-        @pl.when(to_last & (q <= p))
+        @pl.when(to_last & (q <= p) & (q + 2 > p))
         def _():
             remote(outer, outer, zs_r.at[q], z_recv.at[q, 0], {"patch": p + 1}).wait_send()
 
@@ -605,13 +636,28 @@
         def _():
             remote(whole, whole, zs_l.at[q], z_recv.at[q, 0], {"patch": p - 1}).wait_send()
 
-        @pl.when(to_first & (q >= p))
+        @pl.when(to_first & (q >= p) & (q < p + 2))
         def _():
             remote(outer, outer, zs_l.at[q], z_recv.at[q, 0], {"patch": p - 1}).wait_send()
 
     @pl.when(is_end)
     def _():
         guest_copy(0).wait_send()
+
+    far_part = stale_all.at[0, pl.ds(0, group - 1), pl.ds(SHIP, heads - SHIP)]
+
+    @pl.when(to_last)
+    def _():
+        remote(far_part, far_part, zs_r.at[0], z_recv.at[0, 0], {"patch": p + 1}).wait_send()
+        z_straight(False).wait_send()
+
+    @pl.when(to_first)
+    def _():
+        last_q = patches - 1
+        remote(
+            far_part, far_part, zs_l.at[last_q], z_recv.at[0, 0], {"patch": p - 1}
+        ).wait_send()
+        z_straight(True).wait_send()
 
     @pl.when(is_host)
     def _():
@@ -698,10 +744,10 @@
             pltpu.VMEM((SHIP, patch_tok, head_dim), bf),
             pltpu.VMEM((SHIP, 8, patch_tok), f32),
             dma((6,)), dma((K_CHUNKS,)), dma, dma, dma((3,)),
-            dma((patches,)), dma((patches,)), dma((patches, 4)),
+            dma((patches,)), dma((patches,)), dma((patches - 1, 5)),
             dma, dma, dma, dma, dma((K_CHUNKS,)), dma((K_CHUNKS,)), dma, dma,
             dma, dma, dma, dma((later,)), dma, dma, dma, dma((later,)),
-            dma, dma, dma, dma, dma, dma,
+            dma, dma, dma, dma, dma, dma, dma,
         ],
         compiler_params=pltpu.CompilerParams(
             collective_id=0, has_side_effects=True, vmem_limit_bytes=48 * 1024 * 1024
@@ -743,7 +789,7 @@
         and width % (128 * K_CHUNKS) == 0
         and width % (128 * sum(OUT_SPLIT)) == 0
         and width % (TURN * K_CHUNKS) == 0
-        and patches > 3
+        and patches == 4
         and heads > SHIP
         and rows * 4 == head_dim
         and rows * 4 * patches <= 1024

time: 31.8 us -> 31.2 us (0.981)
  Pallas kernels: 31 us -> 30.4 us
    pallas_call x1, Pallas kernels: 30.3 us -> 29.6 us  [fused_device(): pl.pallas_call(functools.partial(fused_kernel, patches=patches), out_shap...]
where the time goes in v5:
time: 31.2 us; the launch traced here: 31.1 us
  Pallas kernels  30.4 us (97%)
  between operations  0.64 us (2%)
    pallas_call x1, Pallas kernels, fused_device(): pl.pallas_call(functools.partial(fused_kernel, patches=patches), out_shap...  29.6 us
    pallas_call x1, Pallas kernels, fused_device(): pl.pallas_call(store_kernel, out_shape=(jax.ShapeDtypeStruct(upd.shape, u...  0.79 us

profile of v5, /device:TPU:0, one launch (start us, length us, event | category | flops | bytes accessed | tf_op | source)
XLA Modules:
  0.0 31.1 jit_solution(6556105418276436744)
XLA Ops:
  0.6 29.6 %shard_map.95 = (bf16[32,3072]{1,0:T(8,128)(2,1)S(1)}, bf16[32,16,256]{2,1,0:T(8,128)(2,1)S(1)}) custom-call(bf16[32,3072]{1,0:T(8,128)(2,1)} %tok_hbm.1, f32[3,3072]{1,0:T(4,128)} %mod_hbm.1, f32[1,128]{1,0:T(1,128)} %bitcast.2, f32[1,128]{1,0:T(1,128)} %bitcast.3, s32[4]{0:T(128)} %lens_hbm.1, bf16[32,16,256]{2,1,0:T(8,128)(2,1)} %st_hbm.1, ...), custom_call_target="tpu_custom_call" | custom-call | tf_op jit(solution)/shard_map/pallas_call | solution.py:707
  30.3 0.8 %shard_map.96 = (bf16[32,3072]{1,0:T(8,128)(2,1)}, bf16[32,16,256]{2,1,0:T(8,128)(2,1)}) custom-call(bf16[32,3072]{1,0:T(8,128)(2,1)S(1)} %get-tuple-element.4.upd, bf16[32,16,256]{2,1,0:T(8,128)(2,1)S(1)} %get-tuple-element.5.cache), custom_call_target="tpu_custom_call" | custom-call | tf_op jit(solution)/shard_map/pallas_call | solution.py:764

commit v6 on v5

--- a/solution.py
+++ b/solution.py
@@ -130,7 +130,7 @@
 
 MESH = pl.DeviceIdType.MESH
 K_CHUNKS = 4
-OUT_SPLIT = (3, 4, 5, 6, 6)
+OUT_SPLIT = (4, 8, 12)
 TURN = 64
 SHIP = 1
 RELAY_ORDER = ((1, 0), (1, 1), (1, 2), (2, 0), (2, 1), (1, 3), (1, 4), (2, 2), (2, 3), (2, 4))

time: 31.2 us -> 30.8 us (0.987)
  Pallas kernels: 30.4 us -> 30 us
    pallas_call x1, Pallas kernels: 29.6 us -> 29.2 us  [fused_device(): pl.pallas_call(functools.partial(fused_kernel, patches=patches), out_shap...]
where the time goes in v6:
time: 30.8 us; the launch traced here: 30.6 us
  Pallas kernels  30 us (97%)
  between operations  0.64 us (2%)
    pallas_call x1, Pallas kernels, fused_device(): pl.pallas_call(functools.partial(fused_kernel, patches=patches), out_shap...  29.2 us
    pallas_call x1, Pallas kernels, fused_device(): pl.pallas_call(store_kernel, out_shape=(jax.ShapeDtypeStruct(upd.shape, u...  0.79 us

profile of v6, /device:TPU:0, one launch (start us, length us, event | category | flops | bytes accessed | tf_op | source)
XLA Modules:
  0.0 30.6 jit_solution(6180348761752037582)
XLA Ops:
  0.6 29.2 %shard_map.95 = (bf16[32,3072]{1,0:T(8,128)(2,1)S(1)}, bf16[32,16,256]{2,1,0:T(8,128)(2,1)S(1)}) custom-call(bf16[32,3072]{1,0:T(8,128)(2,1)} %tok_hbm.1, f32[3,3072]{1,0:T(4,128)} %mod_hbm.1, f32[1,128]{1,0:T(1,128)} %bitcast.2, f32[1,128]{1,0:T(1,128)} %bitcast.3, s32[4]{0:T(128)} %lens_hbm.1, bf16[32,16,256]{2,1,0:T(8,128)(2,1)} %st_hbm.1, ...), custom_call_target="tpu_custom_call" | custom-call | tf_op jit(solution)/shard_map/pallas_call | solution.py:707
  29.8 0.8 %shard_map.96 = (bf16[32,3072]{1,0:T(8,128)(2,1)}, bf16[32,16,256]{2,1,0:T(8,128)(2,1)}) custom-call(bf16[32,3072]{1,0:T(8,128)(2,1)S(1)} %get-tuple-element.4.upd, bf16[32,16,256]{2,1,0:T(8,128)(2,1)S(1)} %get-tuple-element.5.cache), custom_call_target="tpu_custom_call" | custom-call | tf_op jit(solution)/shard_map/pallas_call | solution.py:764
